TPU v7x, 32 devices: a whole 2x2x4 slice. The times are simulated.
32 devices in a mesh: tm: 4 (over x, core), space: 8 (over z, y).
Axes of the slice: x: 2, y: 2, z: 4, core: 2. Of those that a mesh axis runs over, the one named last changes fastest.
Arguments:
- iterate: float32 [64, 16, 3, 4096], P('space', 'tm'), may hold values from -6 to 6
- forcing: float32 [64, 16, 3, 4096], P('space', 'tm'), may hold values from -6 to 6
- initial_velocity: float32 [64, 3, 4096], P('space'), may hold values from -6 to 6
- viscosity: float32 [64, 4096], P('space'), may hold values from 0.1 to 1
- peclet: float32 [64, 3, 4096], P('space'), may hold values from -0.9 to 0.9
- live_patch_mask: int32 [64], P('space'), may hold values from 0 to 1, as said below
- neighbour_holder: int32 [64, 6], P('space'), may hold values from -1 to 7, as said below
- neighbour_slot: int32 [64, 6], P('space'), may hold values from -1 to 7, as said below
Outputs:
- corrected_velocity: float32 [64, 16, 3, 4096], P('space', 'tm')
- corrected_residual: float32 [64, 16, 3, 4096], P('space', 'tm')
Inputs may be any that keep to these rules, and one draw needn't show every extreme that they name: `live_patch_mask`: on each index of space the live slots (1) come first; their count is 2 to 8, and in every draw some two indices j and j + 4 have all 8 slots live. `neighbour_holder`: the patches of one index s of space are the blocks of one aligned 2x2x2 octant; the octant's position is read from the bits of s: bit b of s is bit b div 3 of coordinate b mod 3, except that where a coordinate has two bits its lower bit is complemented when its higher bit is 1; slot p lies at offsets (p mod 2, p div 2 mod 2, p div 4); the entry is -1 where no live patch lies across the face or the slot is dead; the relation is symmetric across opposite faces; the live patches of one index face those of another given index across at most 4 faces, exactly 4 for some pair in every draw. `neighbour_slot`: -1 exactly where neighbour_holder is -1.
All inputs are finite; a program needn't handle non-finite values.
Results may differ from a plain program's by a relative error of at most 0.0003.
Values sent between devices are 32-bit elements; how exact they have to be, the bound alone decides.
A program may use at most 192 MiB of HBM per device.

v0:
```python
import functools
import math

import jax
import jax.numpy as jnp
from jax import lax
from jax.experimental import pallas as pl
from jax.experimental.pallas import tpu as pltpu
from jax.sharding import PartitionSpec as P

WINDOW_SLICES = 16
BLOCK_EDGE = 16
SWEEPS = 5
STEP_DURATION = 0.5
ALPHA_SCALE = 0.1

ROWS = 32
LANES = 128
PAD = 8
TALL = ROWS + 2 * PAD
COMPONENTS = 3
GROUP = 16


def tables():
    n = WINDOW_SLICES
    root = ALPHA_SCALE ** (1.0 / n)
    forward, inverse, diagonals, coupling = [], [[] for _ in range(n)], [], []
    for mode in range(n // 2):
        angle = [2.0 * math.pi * (mode * time % n) / n for time in range(n)]
        alternate = [1.0 - 2.0 * (time % 2) for time in range(n)]
        twist = [root**time for time in range(n)]
        first = [math.cos(angle[t]) * twist[t] for t in range(n)]
        second = [(alternate[t] if mode == 0 else -math.sin(angle[t])) * twist[t] for t in range(n)]
        forward += [first, second]
        for t in range(n):
            back = root ** (-t) / n
            scale = 1.0 if mode == 0 else 2.0
            inverse[t] += [
                scale * math.cos(angle[t]) * back,
                (alternate[t] if mode == 0 else -2.0 * math.sin(angle[t])) * back,
            ]
        real = (1.0 - root * math.cos(2.0 * math.pi * mode / n)) / STEP_DURATION
        diagonals.append((real, (1.0 + root) / STEP_DURATION if mode == 0 else real))
        coupling.append(0.0 if mode == 0 else root * math.sin(2.0 * math.pi * mode / n) / STEP_DURATION)
    return forward, inverse, diagonals, coupling


def insert_bit(rank, dim, bit):
    low = 1 << dim
    return rank // low * (2 * low) + bit * low + rank % low


def remove_bit(slot, dim):
    low = 1 << dim
    return slot // (2 * low) * low + slot % low


def kernel(
    dims,
    weights,
    iterate,
    forcing,
    initial,
    viscosity,
    peclet,
    out_velocity,
    out_residual,
    state,
    residual,
    gathered,
    first_term,
    fields_even,
    fields_odd,
    factor_a,
    factor_b,
    spread,
    update,
    previous,
    res_send,
    res_recv,
    sweep_send,
    sweep_recv,
    send_sem,
    recv_sem,
    local_sem,
):
    time_devices, levels, slots, local = dims
    lead = slots // time_devices
    lead_bits = lead.bit_length() - 1
    fields = (fields_even, fields_odd)
    forward, inverse, diagonals, coupling = tables()
    me = lax.axis_index("tm")
    place = lax.axis_index("space")
    place_bit = [place // (1 << b) % 2 for b in range(levels)]
    rows = lax.broadcasted_iota(jnp.int32, (ROWS, LANES), 0)
    lanes = lax.broadcasted_iota(jnp.int32, (ROWS, LANES), 1)
    odd_row = rows % 2 == 1
    z_index = lanes % BLOCK_EDGE
    y_block = lanes // BLOCK_EDGE

    space_links = []
    for b in range(levels):
        dim = b % 3
        if b + 3 < levels:
            side = 1 - (place_bit[b] + place_bit[b + 3]) % 2
        else:
            side = 1 - place_bit[b]
        partner = place + (1 << b) * (1 - 2 * place_bit[b])
        space_links.append((dim, side, {"space": partner}, 1 + b // 3))
    time_links = []
    for b in range(time_devices.bit_length() - 1):
        bit = me // (1 << b) % 2
        partner = me + (1 << b) * (1 - 2 * bit)
        time_links.append((lead_bits + b, 1 - bit, {"tm": partner}, 0))
    sweep_links = []
    for dim, side, partner, source in space_links:
        if dim >= lead_bits:
            step = 1 << (dim - lead_bits)
            partner = {**partner, "tm": me + step * (1 - 2 * (me // step % 2))}
        sweep_links.append((dim, side, partner, source))
    diagonal = [link[2] for link in sweep_links if len(link[2]) > 1]
    sweep_links += time_links

    barrier = pltpu.get_barrier_semaphore()
    greet = [link[2] for link in space_links]
    greet += diagonal
    greet += [{"tm": lax.rem(me + j, time_devices)} for j in range(1, time_devices)]
    for target in greet:
        pl.semaphore_signal(barrier, inc=1, device_id=target, device_id_type=pl.DeviceIdType.MESH)
    pl.semaphore_wait(barrier, len(greet))

    taken = [0]

    def send(source, target, device):
        number = taken[0]
        taken[0] += 1
        copy = pltpu.make_async_remote_copy(
            src_ref=source,
            dst_ref=target,
            send_sem=send_sem.at[number],
            recv_sem=recv_sem.at[number],
            device_id=device,
            device_id_type=pl.DeviceIdType.MESH,
        )
        copy.start()
        return copy

    def pack(load, count, dim, side, store):
        if dim == 0:
            values = [load(i, PAD + 30 * side, 2) for i in range(count)]
            for i in range(count):
                store(pl.ds(PAD + 2 * i, 2), values[i])
            return
        packed = jnp.zeros((ROWS, LANES), jnp.float32)
        for i in range(count):
            if dim == 1:
                parity = i // 8
                value = load(i, PAD + side - parity, ROWS)
                value = pltpu.roll(value, (i % 8 * BLOCK_EDGE + 128 - 112 * side) % 128, 1)
                chosen = (y_block == i % 8) & (rows % 2 == parity)
            else:
                value = load(i, PAD, ROWS)
                value = pltpu.roll(value, (i + 128 - 15 * side) % 128, 1)
                chosen = z_index == i
            packed = jnp.where(chosen, value, packed)
        store(pl.ds(PAD, ROWS), packed)

    def received(load, i, dim, side):
        if dim == 0:
            return load(PAD + 2 * i, 2)
        if dim == 1:
            value = load(PAD + i // 8 - side, ROWS)
            return pltpu.roll(value, (112 * (1 - side) + 128 - i % 8 * BLOCK_EDGE) % 128, 1)
        return pltpu.roll(load(PAD, ROWS), (15 * side + 128 - i) % 128, 1)

    def beside(load, dim, side):
        if dim == 0:
            return load(PAD + 30 * (1 - side), 2)
        if dim == 1:
            return load(PAD + 1 - 2 * side, ROWS)
        return pltpu.roll(load(PAD, ROWS), (128 - 15 + 30 * side) % 128, 1)

    def source_weights(slot, sources):
        result = []
        for dim, source in sources:
            low, high = weights[slot, dim, source, 0], weights[slot, dim, source, 1]
            if dim == 0:
                result.append((low, high))
            else:
                upper = odd_row if dim == 1 else z_index == 15
                result.append(jnp.where(upper, high, low))
        return result

    def fill_ends(channels, ghosts_of, weighted):
        ends = []
        for i in range(len(channels)):
            low = high = None
            for value, (low_weight, high_weight) in zip(ghosts_of(i), weighted):
                low = low_weight * value if low is None else low + low_weight * value
                high = high_weight * value if high is None else high + high_weight * value
            ends.append((low, high))
        for field, (low, high) in zip(channels, ends):
            field[pl.ds(PAD - 2, 2), :] = low
            field[pl.ds(PAD + ROWS, 2), :] = high

    def adjacent(field, coefficients, ghosts):
        beyond = [None] * 3
        for dim, value, weight in ghosts:
            term = value * weight
            beyond[dim] = term if beyond[dim] is None else beyond[dim] + term
        value = field[pl.ds(PAD, ROWS), :]
        total = coefficients[0] * field[pl.ds(PAD + 2, ROWS), :]
        total = total + coefficients[1] * field[pl.ds(PAD - 2, ROWS), :]
        y_up = jnp.where(odd_row, beyond[1], field[pl.ds(PAD + 1, ROWS), :])
        y_up = pltpu.roll(jnp.where(y_block == 0, y_up, value), 112, 1)
        y_low = jnp.where(odd_row, field[pl.ds(PAD - 1, ROWS), :], beyond[1])
        y_low = pltpu.roll(jnp.where(y_block == 7, y_low, value), 16, 1)
        total = total + coefficients[2] * y_up + coefficients[3] * y_low
        z_up = jnp.where(z_index == 15, beyond[2], pltpu.roll(value, 127, 1))
        z_low = jnp.where(z_index == 0, beyond[2], pltpu.roll(value, 1, 1))
        return value, total + coefficients[4] * z_up + coefficients[5] * z_low

    def coefficients_of(slot):
        result = []
        for dim in range(3):
            number = peclet[slot, dim]
            result += [1.0 - number, 1.0 + number]
        return result

    def state_channel(i):
        return i // local, i % local

    def start_residual(phase):
        copies = []
        shift = send(
            state.at[:, :, local - 1, pl.ds(PAD, ROWS), :],
            previous.at[phase],
            {"tm": lax.rem(me + 1, time_devices)},
        )
        for number, (dim, side, partner, source) in enumerate(space_links):
            def one_slot(rank, carry, dim=dim, side=side, number=number):
                slot = insert_bit(rank, dim, side)

                def load(i, offset, size):
                    c, j = state_channel(i)
                    return state[c, slot, j, pl.ds(offset, size), :]

                def store(where, value):
                    res_send[phase, number, rank, where, :] = value

                pack(load, COMPONENTS * local, dim, side, store)
                return carry

            lax.fori_loop(0, slots // 2, one_slot, 0)
            copies.append(send(res_send.at[phase, number], res_recv.at[phase, number], partner))
        return shift, copies

    def residual_of(phase, c, store):
        def one_slot(slot, carry):
            coefficients = coefficients_of(slot)
            thickness = viscosity[slot]
            live = weights[slot, 0, 0, 2]
            bits = [slot // (1 << dim) % 2 for dim in range(3)]
            sources = [(dim, 0) for dim in range(3)]
            sources += [(dim, source) for dim, side, partner, source in space_links]
            weighted = source_weights(slot, sources)

            def ghosts_of(j, wanted):
                i = c * local + j
                found = []
                for dim in range(3):
                    if dim not in wanted:
                        continue
                    other = slot + (1 << dim) * (1 - 2 * bits[dim])
                    load = lambda offset, size: state[c, other, j, pl.ds(offset, size), :]
                    found.append((dim, beside(load, dim, 1 - bits[dim]), weighted[dim]))
                for number, (dim, side, partner, source) in enumerate(space_links):
                    if dim not in wanted:
                        continue
                    rank = remove_bit(slot, dim)
                    load = lambda offset, size: res_recv[
                        phase, number, rank, pl.ds(offset, size), :
                    ]
                    found.append((dim, received(load, i, dim, side), weighted[3 + number]))
                return found

            fill_ends(
                [state.at[c, slot, j] for j in range(local)],
                lambda j: [value for _, value, _ in ghosts_of(j, (0,))],
                [w for (dim, _), w in zip(sources, weighted) if dim == 0],
            )
            for j in range(local):
                value, total = adjacent(state.at[c, slot, j], coefficients, ghosts_of(j, (1, 2)))
                if j == 0:
                    earlier = jnp.where(me == 0, initial[c, :, slot, :], previous[phase, c, slot])
                else:
                    earlier = state[c, slot, j - 1, pl.ds(PAD, ROWS), :]
                answer = forcing[slot, c, :, j, :] - (value - earlier) / STEP_DURATION
                answer = (answer - thickness * (6.0 * value - total)) * live
                store(slot, j, answer)
            return carry

        lax.fori_loop(0, slots, one_slot, 0)

    def take(slot, carry):
        for j in range(local):
            for c in range(COMPONENTS):
                state[c, slot, j, pl.ds(PAD, ROWS), :] = iterate[slot, c, :, j, :]
        return carry

    lax.fori_loop(0, slots, take, 0)
    shift, copies = start_residual(0)
    pending = [*copies]

    def make_factors(p, carry):
        slot = me * lead + p
        diffusion = 6.0 * viscosity[slot]
        for mode in range(GROUP // 2):
            real, second = diagonals[mode]
            if mode == 0:
                factor_a[p, mode] = 1.0 / (real + diffusion)
                factor_b[p, mode] = 1.0 / (second + diffusion)
            else:
                diagonal = real + diffusion
                determinant = diagonal * diagonal + coupling[mode] * coupling[mode]
                factor_a[p, mode] = diagonal / determinant
                factor_b[p, mode] = coupling[mode] / determinant
        return carry

    lax.fori_loop(0, lead, make_factors, 0)

    shift.wait()
    for copy in copies:
        copy.wait_recv()

    def exchange_time(source, target, number):
        moved = []
        for j in range(1, time_devices):
            peer = lax.rem(me + j, time_devices)
            moved.append(send(source(peer), target, {"tm": peer}))
        own = pltpu.make_async_copy(source(me), target, local_sem.at[number])
        own.start()
        return moved, own

    arrivals = []
    for c in range(COMPONENTS):
        def keep(slot, j, value, c=c):
            residual[c, slot, j] = value

        residual_of(0, c, keep)
        arrivals.append(
            exchange_time(
                lambda peer, c=c: residual.at[c, pl.ds(peer * lead, lead)], gathered.at[c, me], c
            )
        )

    def start_sweep(turn, c):
        copies = []
        for number, (dim, side, partner, source) in enumerate(sweep_links):
            inside = dim < lead_bits
            count = lead // 2 if inside else lead

            def one_slot(rank, carry, dim=dim, side=side, number=number, inside=inside):
                p = insert_bit(rank, dim, side) if inside else rank

                def load(i, offset, size):
                    return fields[turn % 2][c, p, i, pl.ds(offset, size), :]

                def store(where, value):
                    sweep_send[turn, c, number, rank, where, :] = value

                pack(load, GROUP, dim, side, store)
                return carry

            lax.fori_loop(0, count, one_slot, 0)
            copies.append(
                send(
                    sweep_send.at[turn, c, number, pl.ds(0, count)],
                    sweep_recv.at[turn, c, number, pl.ds(0, count)],
                    partner,
                )
            )
        pending.extend(copies)
        return copies

    sweeps = []
    for c in range(COMPONENTS):
        moved, own = arrivals[c]
        for copy in moved:
            copy.wait_recv()
        own.wait()
        pending.extend(moved)

        def transform(step, carry, c=c):
            p, chunk = step // (ROWS // 8), step % (ROWS // 8)
            at = pl.multiple_of(chunk * 8, 8)
            times = [
                gathered[c, t, p, j, pl.ds(at, 8), :] for t in range(time_devices) for j in range(local)
            ]
            for mode in range(GROUP // 2):
                sums = []
                for row in (forward[2 * mode], forward[2 * mode + 1]):
                    total = row[0] * times[0]
                    for t in range(1, WINDOW_SLICES):
                        if abs(row[t]) > 1e-12:
                            total = total + row[t] * times[t]
                    sums.append(total)
                a = factor_a[p, mode, pl.ds(at, 8), :]
                b = factor_b[p, mode, pl.ds(at, 8), :]
                if mode == 0:
                    real, imag = a * sums[0], b * sums[1]
                else:
                    real, imag = a * sums[0] + b * sums[1], a * sums[1] - b * sums[0]
                for part, value in ((0, real), (1, imag)):
                    first_term[c, p, 2 * mode + part, pl.ds(at, 8), :] = value
                    fields_even[c, p, 2 * mode + part, pl.ds(PAD + at, 8), :] = value
            return carry

        lax.fori_loop(0, lead * (ROWS // 8), transform, 0)
        sweeps.append(start_sweep(0, c))

    returns = []
    for turn in range(SWEEPS - 1):
        for c in range(COMPONENTS):
            for copy in sweeps[c]:
                copy.wait_recv()

            def one_slot(p, carry, turn=turn, c=c):
                slot = me * lead + p
                coefficients = coefficients_of(slot)
                thickness = viscosity[slot]

                now, after = fields[turn % 2], fields[(turn + 1) % 2]
                sources = [(dim, 0) for dim in range(lead_bits)]
                sources += [(dim, source) for dim, side, partner, source in sweep_links]
                weighted = source_weights(slot, sources)

                def ghosts_of(i, wanted):
                    found = []
                    for dim in range(lead_bits):
                        if dim not in wanted:
                            continue
                        bit = p // (1 << dim) % 2
                        other = p + (1 << dim) * (1 - 2 * bit)
                        load = lambda offset, size: now[c, other, i, pl.ds(offset, size), :]
                        found.append((dim, beside(load, dim, 1 - bit), weighted[dim]))
                    for number, (dim, side, partner, source) in enumerate(sweep_links):
                        if dim not in wanted:
                            continue
                        rank = remove_bit(p, dim) if dim < lead_bits else p
                        load = lambda offset, size: sweep_recv[
                            turn, c, number, rank, pl.ds(offset, size), :
                        ]
                        found.append((dim, received(load, i, dim, side), weighted[lead_bits + number]))
                    return found

                fill_ends(
                    [now.at[c, p, i] for i in range(GROUP)],
                    lambda i: [value for _, value, _ in ghosts_of(i, (0,))],
                    [w for (dim, _), w in zip(sources, weighted) if dim == 0],
                )

                def one_channel(i):
                    _, total = adjacent(now.at[c, p, i], coefficients, ghosts_of(i, (1, 2)))
                    return thickness * total

                for mode in range(GROUP // 2):
                    real = one_channel(2 * mode)
                    imag = one_channel(2 * mode + 1)
                    a, b = factor_a[p, mode], factor_b[p, mode]
                    if mode == 0:
                        real, imag = a * real, b * imag
                    else:
                        real, imag = a * real + b * imag, a * imag - b * real
                    for part, change in ((0, real), (1, imag)):
                        after[c, p, 2 * mode + part, pl.ds(PAD, ROWS), :] = (
                            first_term[c, p, 2 * mode + part] + change
                        )
                return carry

            lax.fori_loop(0, lead, one_slot, 0)
            if turn < SWEEPS - 2:
                sweeps[c] = start_sweep(turn + 1, c)
                continue

            def back(step, carry, c=c):
                p, chunk = step // (ROWS // 8), step % (ROWS // 8)
                at = pl.multiple_of(chunk * 8, 8)
                modes = [
                    fields[(SWEEPS - 1) % 2][c, p, i, pl.ds(PAD + at, 8), :] for i in range(GROUP)
                ]
                for time in range(WINDOW_SLICES):
                    row = inverse[time]
                    total = row[0] * modes[0]
                    for i in range(1, GROUP):
                        if abs(row[i]) > 1e-12:
                            total = total + row[i] * modes[i]
                    spread[c, time // local, p, time % local, pl.ds(at, 8), :] = total
                return carry

            lax.fori_loop(0, lead * (ROWS // 8), back, 0)
            returns.append(
                exchange_time(
                    lambda peer, c=c: spread.at[c, peer],
                    update.at[c, pl.ds(me * lead, lead)],
                    COMPONENTS + c,
                )
            )

    for c in range(COMPONENTS):
        moved, own = returns[c]
        for copy in moved:
            copy.wait_recv()
        own.wait()
        pending.extend(moved)

        def correct(slot, carry, c=c):
            for j in range(local):
                value = state[c, slot, j, pl.ds(PAD, ROWS), :] + update[c, slot, j]
                state[c, slot, j, pl.ds(PAD, ROWS), :] = value
                out_velocity[slot, c, :, j, :] = value
            return carry

        lax.fori_loop(0, slots, correct, 0)

    shift, copies = start_residual(1)
    pending.extend(copies)
    for copy in copies:
        copy.wait_recv()
    shift.wait()
    for c in range(COMPONENTS):
        def give(slot, j, value, c=c):
            out_residual[slot, c, :, j, :] = value

        residual_of(1, c, give)
    for copy in pending:
        copy.wait_send()


def body(
    iterate,
    forcing,
    initial_velocity,
    viscosity,
    peclet,
    live_patch_mask,
    neighbour_holder,
    neighbour_slot,
):
    time_devices = lax.axis_size("tm")
    levels = lax.axis_size("space").bit_length() - 1
    slots, local = iterate.shape[:2]
    lead = slots // time_devices
    place = lax.axis_index("space")

    holder = neighbour_holder.reshape(slots, 3, 2)
    depth = 1 + max(1, (levels + 2) // 3)
    sources = []
    for source in range(depth):
        per_dim = []
        for dim in range(3):
            b = dim + 3 * (source - 1)
            if source == 0:
                found = holder[:, dim] == place
            elif b < levels:
                found = holder[:, dim] == (place ^ (1 << b))
            else:
                found = jnp.zeros((slots, 2), bool)
            per_dim.append(found)
        sources.append(jnp.stack(per_dim, axis=1))
    weights = jnp.stack(sources, axis=2).astype(jnp.float32)
    live = jnp.broadcast_to(
        live_patch_mask.astype(jnp.float32)[:, None, None, None], (slots, 3, depth, 1)
    )
    weights = jnp.concatenate([weights, live], axis=3)

    def by_rows(array):
        split = array.reshape(array.shape[:-1] + (ROWS, LANES))
        return split.transpose((0, 2, 3, 1, 4) if split.ndim == 5 else (1, 2, 0, 3))

    def whole(array):
        return array.transpose(0, 3, 1, 2, 4).reshape(slots, local, COMPONENTS, ROWS * LANES)

    time_bits = time_devices.bit_length() - 1
    links = levels + time_bits
    turns = SWEEPS - 1
    copies = 2 * (1 + levels) + 2 * COMPONENTS * (time_devices - 1) + turns * COMPONENTS * links
    f32 = jnp.float32
    blocks = (ROWS, LANES)
    tall = (TALL, LANES)
    result = jax.ShapeDtypeStruct((slots, COMPONENTS, ROWS, local, LANES), f32)
    velocity, residual = pl.pallas_call(
        functools.partial(kernel, (time_devices, levels, slots, local)),
        out_shape=(result, result),
        in_specs=[pl.BlockSpec(memory_space=pltpu.SMEM)]
        + [pl.BlockSpec(memory_space=pltpu.VMEM)] * 5,
        out_specs=[pl.BlockSpec(memory_space=pltpu.VMEM)] * 2,
        scratch_shapes=[
            pltpu.VMEM((COMPONENTS, slots, local) + tall, f32),
            pltpu.VMEM((COMPONENTS, slots, local) + blocks, f32),
            pltpu.VMEM((COMPONENTS, time_devices, lead, local) + blocks, f32),
            pltpu.VMEM((COMPONENTS, lead, GROUP) + blocks, f32),
            pltpu.VMEM((COMPONENTS, lead, GROUP) + tall, f32),
            pltpu.VMEM((COMPONENTS, lead, GROUP) + tall, f32),
            pltpu.VMEM((lead, GROUP // 2) + blocks, f32),
            pltpu.VMEM((lead, GROUP // 2) + blocks, f32),
            pltpu.VMEM((COMPONENTS, time_devices, lead, local) + blocks, f32),
            pltpu.VMEM((COMPONENTS, slots, local) + blocks, f32),
            pltpu.VMEM((2, COMPONENTS, slots) + blocks, f32),
            pltpu.VMEM((2, levels, slots // 2) + tall, f32),
            pltpu.VMEM((2, levels, slots // 2) + tall, f32),
            pltpu.VMEM((turns, COMPONENTS, links, lead) + tall, f32),
            pltpu.VMEM((turns, COMPONENTS, links, lead) + tall, f32),
            pltpu.SemaphoreType.DMA((copies,)),
            pltpu.SemaphoreType.DMA((copies,)),
            pltpu.SemaphoreType.DMA((2 * COMPONENTS,)),
        ],
        compiler_params=pltpu.CompilerParams(
            collective_id=0, has_side_effects=True, vmem_limit_bytes=60 * 1024 * 1024
        ),
    )(
        weights,
        by_rows(iterate),
        by_rows(forcing),
        by_rows(initial_velocity),
        viscosity.reshape((slots,) + blocks),
        peclet.reshape((slots, 3) + blocks),
    )
    return whole(velocity), whole(residual)


def solution(mesh):
    return jax.shard_map(
        body,
        mesh=mesh,
        in_specs=(
            P("space", "tm", None, None),
            P("space", "tm", None, None),
            P("space", None, None),
            P("space", None),
            P("space", None, None),
            P("space"),
            P("space", None),
            P("space", None),
        ),
        out_specs=(P("space", "tm", None, None), P("space", "tm", None, None)),
        check_vma=False,
    )
```

profile of v0, /device:TPU:0, one launch (start us, length us, event | category | flops | bytes accessed | tf_op | source)
XLA Modules:
  0.0 122.9 jit_solution(15762428812786083070)
XLA Ops:
  0.6 0.7 convert_element_type.7
  1.3 0.8 copy.32
  2.2 0.1 copy.36
  2.3 0.1 broadcast_in_dim.2
  2.3 0.7 pad_maximum_fusion.weights
  3.0 1.6 %copy.46 = f32[1,8,32,128]{3,2,1,0:T(8,128)} copy(f32[1,8,32,128]{3,1,2,0:T(8,128)} %bitcast.43) | data formatting | bytes 262144
  4.6 1.1 copy.45
  5.7 0.8 copy.37.peclet
  6.5 112.4 %shard_map.86 = (f32[8,3,32,4,128]{4,3,2,1,0:T(4,128)}, f32[8,3,32,4,128]{4,3,2,1,0:T(4,128)}) custom-call(f32[8,3,2,3]{3,2,1,0:T(2,128)} %pad_maximum_fusion.weights, f32[8,3,32,4,128]{4,3,2,1,0:T(4,128)} %bitcast.38, f32[8,3,32,4,128]{4,3,2,1,0:T(4,128)} %bitcast.39, f32[3,32,8,128]{3,2,1,0:T(8,128)} %bitcast.42, f32[8,32,128]{2,1,0:T(8,128)} %bitcast.40, ...), custom_call_target="tpu_custom_call" | custom-call | tf_op jit(solution)/shard_map/pallas_call | solution.py:593
  118.9 0.0 copy-start
  118.9 2.8 %copy.51 = f32[8,4,3,4096]{3,1,2,0:T(4,128)} copy(f32[8,4,3,4096]{3,1,2,0:T(4,128)} %bitcast.36) | data formatting | bytes 3145728
  121.7 0.0 copy-done
  121.7 1.1 copy.52
  (7 shorter events, 0.1 us)
Async XLA Ops:
  118.9 2.8 %copy-start = (f32[8,3,32,4,128]{4,3,2,1,0:T(4,128)S(1)}, f32[8,3,32,4,128]{4,3,2,1,0:T(4,128)}, u32[]{:S(2)}) copy-start(f32[8,3,32,4,128]{4,3,2,1,0:T(4,128)} %get-tuple-element.5) | copy-start | bytes 4718596
where the time goes:
time: 123 us
  Pallas kernels  112 us (91%)
  local copies, waits for them, and re-layouts  8.37 us (7%)
  other arithmetic  1.39 us (1%)
    pallas_call x1, Pallas kernels, body(): pl.pallas_call(functools.partial(kernel, (time_devices, levels, slots, lo...  112 us
    unnamed x7, local copies, waits for them, and re-layouts  7.38 us

commit v1 on v0

v1 whole, which is shorter than its diff:
```python
import functools

import jax
import jax.numpy as jnp
from jax import lax
from jax.experimental import pallas as pl
from jax.experimental.pallas import tpu as pltpu
from jax.sharding import PartitionSpec as P

BLOCK_EDGE = 16
SWEEPS = 5
ALPHA_SCALE = 0.1

ROWS = 32
LANES = 128
COMPONENTS = 3
PLANES = BLOCK_EDGE
CELLS = PLANES * 8
TALL = CELLS + 24
WIDE = CELLS + 8
UNROLL = 4


def kernel(
    dims,
    holder,
    live,
    iterate,
    forcing,
    initial,
    viscosity,
    peclet,
    out_velocity,
    out_residual,
    stage_iterate,
    stage_forcing,
    field,
    local_field,
    source,
    force,
    start,
    ghost_y,
    ghost_z,
    coefficient,
    power,
    scale,
    gain,
    offset,
    carry_in,
    present,
    x_send,
    x_recv,
    y_send,
    y_recv,
    z_send,
    z_recv,
    x_end,
    y_end,
    z_end,
    end_recv,
    x_gain,
    y_gain,
    z_gain,
    x_offset,
    y_offset,
    z_offset,
    x_old,
    y_old,
    z_old,
    send_sem,
    recv_sem,
    stage_send,
    stage_recv,
    stage_local,
):
    chips, levels, slots, local = dims
    half = slots // 2
    times = 2 * local
    per_block = 2 * half
    me = lax.axis_index("tm")
    place = lax.axis_index("space")
    chip, core = me // 2, me % 2
    power_message = COMPONENTS * (SWEEPS + 1)

    sub = lax.broadcasted_iota(jnp.int32, (8, LANES), 0)
    lane = lax.broadcasted_iota(jnp.int32, (8, LANES), 1)
    z_index = lane % BLOCK_EDGE
    y_block = lane // BLOCK_EDGE
    y_upper = sub // half == 1
    slot_index = sub % half
    second = slot_index // 2 == 1
    first_block, last_block = y_block == 0, y_block == 7
    z_first, z_last = z_index == 0, z_index == BLOCK_EDGE - 1
    low_inner = (~y_upper) & second
    high_inner = y_upper & (~second)
    flat_lane = lax.broadcasted_iota(jnp.int32, (times, LANES), 1) // BLOCK_EDGE

    place_bit = [place // (1 << b) % 2 for b in range(levels)]

    def links_of(dim):
        found = []
        if dim < levels:
            side = 1 - place_bit[dim]
            if dim + 3 < levels:
                side = 1 - (place_bit[dim] + place_bit[dim + 3]) % 2
            found.append((side, place + (1 << dim) * (1 - 2 * place_bit[dim])))
            if dim + 3 < levels:
                far = dim + 3
                found.append((1 - side, place + (1 << far) * (1 - 2 * place_bit[far])))
        return found

    x_links, y_links, z_links = links_of(0), links_of(1), links_of(2)

    def seat(jump, which):
        return lax.rem(chip + jump, chips) * 2 + which

    greet = [{"tm": seat(j, core)} for j in range(1, chips)]
    for side, partner in x_links + y_links:
        greet += [{"space": partner, "tm": seat(j, core)} for j in range(chips)]
    greet += [{"tm": seat(j, 1 - core)} for j in range(chips)]
    for side, partner in z_links:
        greet += [{"space": partner, "tm": seat(j, 1 - core)} for j in range(chips)]
    barrier = pltpu.get_barrier_semaphore()
    for target in greet:
        pl.semaphore_signal(barrier, inc=1, device_id=target, device_id_type=pl.DeviceIdType.MESH)
    pl.semaphore_wait(barrier, len(greet))

    def remote(src, dst, sems, number, device):
        return pltpu.make_async_remote_copy(
            src_ref=src,
            dst_ref=dst,
            send_sem=sems[0].at[number],
            recv_sem=sems[1].at[number],
            device_id=device,
            device_id_type=pl.DeviceIdType.MESH,
        )

    peer = {"tm": seat(0, 1 - core)}
    mine = pl.ds(core * half, half)
    theirs = pl.ds((1 - core) * half, half)
    stage = (stage_send, stage_recv)
    swaps, owns = [], []
    for c in range(COMPONENTS):
        swaps.append(
            remote(iterate.at[theirs, c], stage_iterate.at[core, :, c], stage, c, peer)
        )
        owns.append(
            pltpu.make_async_copy(
                iterate.at[mine, c], stage_iterate.at[core, :, c], stage_local.at[c]
            )
        )
    for c in range(COMPONENTS):
        swaps.append(
            remote(forcing.at[theirs, c], stage_forcing.at[core, :, c], stage, COMPONENTS + c, peer)
        )
        owns.append(
            pltpu.make_async_copy(
                forcing.at[mine, c], stage_forcing.at[core, :, c], stage_local.at[COMPONENTS + c]
            )
        )
    for copy in swaps + owns:
        copy.start()

    per_message = (chips - 1) + chips * (len(x_links) + len(y_links) + 1 + len(z_links))

    def copies(message, buffer, pitch, base, c, carried=True):
        sems = (send_sem, recv_sem)
        number = [message * per_message]
        found = []

        def add(src, dst, device, condition=None):
            found.append((remote(src, dst, sems, number[0], device), condition))
            number[0] = number[0] + 1

        extra = range(1, chips) if carried else ()
        for n, (side, partner) in enumerate(x_links):
            add(x_send.at[message, n], x_recv.at[message, n], {"space": partner})
        for n, (side, partner) in enumerate(y_links):
            add(y_send.at[message, n], y_recv.at[message, n], {"space": partner})
        for side, partner in z_links:
            add(
                z_send.at[message, core],
                z_recv.at[message, 1 - core],
                {"space": partner, "tm": seat(0, 1 - core)},
                core == side,
            )
        add(z_send.at[message, 1 - core], z_recv.at[message, core], peer)
        for j in extra:
            last = pl.ds((times - 1) * pitch + base, CELLS)
            add(buffer.at[c, last], end_recv.at[message, j - 1], {"tm": seat(j, core)})
            for n, (side, partner) in enumerate(x_links):
                add(
                    x_send.at[message, n, pl.ds(times * 4, 8)],
                    x_end.at[message, n, j - 1],
                    {"space": partner, "tm": seat(j, core)},
                )
            for n, (side, partner) in enumerate(y_links):
                add(
                    y_send.at[message, n, pl.ds(32, 8)],
                    y_end.at[message, n, j - 1],
                    {"space": partner, "tm": seat(j, core)},
                )
            end = pl.ds((times - 1) * 8, 8)
            for side, partner in z_links:
                add(
                    z_send.at[message, core, end],
                    z_end.at[message, 1 - core, j - 1],
                    {"space": partner, "tm": seat(j, 1 - core)},
                    core == side,
                )
            add(
                z_send.at[message, 1 - core, end],
                z_end.at[message, core, j - 1],
                {"tm": seat(j, 1 - core)},
            )
        return found

    def start_all(found):
        for copy, condition in found:
            if condition is None:
                copy.start()
            else:
                pl.when(condition)(copy.start)

    def wait_all(found):
        for copy, condition in found:
            if condition is None:
                copy.wait()
            else:
                pl.when(condition)(copy.wait)

    outer_known = functools.reduce(
        jnp.logical_or, [core == side for side, partner in z_links], jnp.bool_(False)
    )

    def pack(message, load, pitch, base):
        for n, (side, partner) in enumerate(x_links):
            for t in range(times):
                value = load(pl.ds(t * pitch + base + side * (CELLS - 7), 4, stride=2))
                x_send[message, n, pl.ds(4 * t, 4), :] = value
            x_send[message, n, pl.ds(4 * times, 4), :] = value
            x_send[message, n, pl.ds(4 * times + 4, 4), :] = value
        for n, (side, partner) in enumerate(y_links):
            for k in range(4):
                total = None
                for i in range(8):
                    row = base + ((k % 2) * 8 + i) * 8 + k // 2 + side * 6
                    value = load(pl.ds(row, times, stride=pitch))
                    value = pltpu.roll(value, lax.rem(BLOCK_EDGE * i + 128 - 112 * side, 128), 1)
                    total = value if total is None else jnp.where(flat_lane == i, value, total)
                y_send[message, n, pl.ds(8 * k, times), :] = total
                y_send[message, n, pl.ds(32 + k, 1), :] = total[times - 1 : times]
                y_send[message, n, pl.ds(36 + k, 1), :] = total[times - 1 : times]
        for t in range(times):
            low = high = None
            for x in range(PLANES):
                value = load(pl.ds(t * pitch + base + 8 * x, 8))
                value = pltpu.roll(value, (x - 15) % 128, 1)
                high = value if high is None else jnp.where(z_index == x, value, high)
                low = value if low is None else jnp.where(z_index == (x + 1) % 16, value, low)
            z_send[message, 1, pl.ds(8 * t, 8), :] = high
            z_send[message, 0, pl.ds(8 * t, 8), :] = pltpu.roll(low, 15, 1)

    wraps = [jnp.where(chip - j < 0, ALPHA_SCALE, 1.0) for j in range(1, chips + 1)]
    keeps = [
        jnp.where(lax.rem(chip - j + chips, chips) == chips - 1, 0.0, 1.0)
        for j in range(1, chips + 1)
    ]

    def gains_of(ratio):
        powers = [jnp.ones_like(ratio)]
        for j in range(chips):
            powers.append(powers[-1] * ratio)
        scaled = 1.0 / (1.0 - ALPHA_SCALE * powers[chips])
        return [wraps[j] * (powers[j] * scaled) for j in range(chips)]

    def combine(gains, ends, weights=None):
        total = None
        for j in range(chips):
            term = gains[j] * ends[j]
            if weights is not None:
                term = term * weights[j]
            total = term if total is None else total + term
        return total

    def x_ends(message, n):
        found = [x_end[message, n, j, pl.ds(0, 4), :] for j in range(chips - 1)]
        return found + [x_recv[message, n, pl.ds(4 * times, 4), :]]

    def y_ends(message, n):
        found = [y_end[message, n, j, pl.ds(0, 4), :] for j in range(chips - 1)]
        return found + [y_recv[message, n, pl.ds(32, 4), :]]

    def z_ends(message, side):
        found = [z_end[message, side, j] for j in range(chips - 1)]
        return found + [z_recv[message, side, pl.ds(8 * (times - 1), 8), :]]

    def ghosts(message, c, mode):
        def finish(value, old, index):
            if mode == "raw":
                return value
            if mode == "last":
                return value - old[index]
            old[index] = value
            return value

        for t in range(times):
            base = t * TALL
            field[c, pl.ds(base, 8), :] = field[c, pl.ds(base + CELLS - 1, 8), :]
            field[c, pl.ds(base + CELLS + 8, 8), :] = field[c, pl.ds(base + 9, 8), :]
        for n, (side, partner) in enumerate(x_links):
            if mode == "raw":
                x_offset[c, n] = combine(
                    [x_gain[n, j] for j in range(chips)], x_ends(message, n), keeps
                )
            else:
                added = combine([x_gain[n, j] for j in range(chips)], x_ends(message, n))
                added = added + x_offset[c, n]
            for t in range(times):
                at = pl.ds(4 * t, 4)
                value = x_recv[message, n, at, :]
                if mode != "raw":
                    value = value + x_recv[power_message, n, at, :] * added
                value = finish(value, x_old, (c, n, at, slice(None)))
                field[c, pl.ds(t * TALL + side * (CELLS + 9), 4, stride=2), :] = value
        for n, (side, partner) in enumerate(y_links):
            if mode == "raw":
                y_offset[c, n] = combine(
                    [y_gain[n, j] for j in range(chips)], y_ends(message, n), keeps
                )
            else:
                added = combine([y_gain[n, j] for j in range(chips)], y_ends(message, n))
                added = added + y_offset[c, n]
            for k in range(4):
                at = pl.ds(8 * k, times)
                value = y_recv[message, n, at, :]
                if mode != "raw":
                    value = value + y_recv[power_message, n, at, :] * added[k : k + 1]
                value = finish(value, y_old, (c, n, at, slice(None)))
                for i in range(8):
                    turned = pltpu.roll(
                        value, lax.rem(112 * (1 - side) + 128 - BLOCK_EDGE * i, 128), 1
                    )
                    row = ((k % 2) * 8 + i) * 8 + k // 2 + side * 6
                    ghost_y[c, pl.ds(row, times, stride=WIDE), :] = turned
        added = [None, None]
        for side in range(2):
            ends = z_ends(message, side)
            gains = [z_gain[side, j] for j in range(chips)]
            if mode == "raw":
                z_offset[c, side] = combine(gains, ends, keeps)
            else:
                added[side] = combine(gains, ends) + z_offset[c, side]
        even = z_index % 2 == 0
        for t in range(times):
            at = pl.ds(8 * t, 8)
            pair = []
            for side in range(2):
                value = z_recv[message, side, at, :]
                if mode != "raw":
                    value = value + z_recv[power_message, side, at, :] * added[side]
                value = jnp.where((core != side) | outer_known, value, 0.0)
                pair.append(finish(value, z_old, (c, side, at, slice(None))))
            low, high = pair[0], pltpu.roll(pair[1], 15, 1)
            ghost_z[c, pl.ds(16 * t, 8), :] = jnp.where(even, low, high)
            ghost_z[c, pl.ds(16 * t + 8, 8), :] = jnp.where(even, high, low)

    def stencil(c, t, x, row, parity, factors):
        base = t * TALL + 8 + row

        def load(shift):
            return field[c, pl.ds(base + shift, 8), :]

        value = load(0)
        total = factors[0] * load(-8) + factors[1] * load(8)
        beyond = ghost_y[c, pl.ds(t * WIDE + row, 8), :]
        low = jnp.where(y_upper, load(-4), jnp.where(low_inner, load(2), beyond))
        low = pltpu.roll(jnp.where(last_block, low, value), 16, 1)
        high = jnp.where(y_upper, jnp.where(high_inner, load(-2), beyond), load(4))
        high = pltpu.roll(jnp.where(first_block, high, value), 112, 1)
        total = total + factors[2] * low + factors[3] * high
        edge = ghost_z[c, pl.ds(16 * t + 8 * parity, 8), :]
        edge = pltpu.roll(edge, lax.rem(128 - x, 128), 1)
        low = jnp.where(z_first, edge, pltpu.roll(value, 1, 1))
        high = jnp.where(z_last, edge, pltpu.roll(value, 127, 1))
        return value, total + factors[4] * low + factors[5] * high

    def over_planes(body):
        def one(group, carry):
            for i in range(UNROLL):
                x = group * UNROLL + i
                body(x, pl.multiple_of(x * 8, 8), i % 2)
            return carry

        lax.fori_loop(0, PLANES // UNROLL, one, 0)

    def factors_at(row):
        return [coefficient[f, pl.ds(row, 8), :] for f in range(6)]

    def sweep(c):
        def plane(x, row, parity):
            factors = factors_at(row)
            ratio = power[pl.ds(row, 8), :]
            before = None
            for t in range(times):
                _, total = stencil(c, t, x, row, parity, factors)
                total = total + source[c, pl.ds(t * CELLS + row, 8), :]
                if before is not None:
                    total = total + ratio * before
                local_field[c, pl.ds(t * WIDE + row, 8), :] = total
                before = total

        over_planes(plane)

    def first_residual(c):
        def plane(x, row, parity):
            factors = factors_at(row)
            ratio = power[pl.ds(row, 8), :]
            inverse = scale[pl.ds(row, 8), :]
            alive = present[6]
            earlier = jnp.where(chip == 0, start[c, pl.ds(row, 8), :], 0.0)
            before = None
            for t in range(times):
                value, total = stencil(c, t, x, row, parity, factors)
                total = total + inverse * force[c, pl.ds(t * CELLS + row, 8), :]
                total = (total + (ratio * earlier - value)) * alive
                source[c, pl.ds(t * CELLS + row, 8), :] = total
                if before is not None:
                    total = total + ratio * before
                local_field[c, pl.ds(t * WIDE + row, 8), :] = total
                before, earlier = total, value

        over_planes(plane)

    def own_ends(message, c, row):
        found = [end_recv[message, j, pl.ds(row, 8), :] for j in range(chips - 1)]
        return found

    def first_offset(message, c):
        def plane(x, row, parity):
            ends = own_ends(message, c, row)
            ends.append(field[c, pl.ds((times - 1) * TALL + 8 + row, 8), :])
            gains = [gain[j, pl.ds(row, 8), :] for j in range(chips)]
            offset[c, pl.ds(row, 8), :] = combine(gains, ends, keeps) * present[6]

        over_planes(plane)

    def complete(message, c, last):
        def plane(x, row, parity):
            ends = own_ends(message, c, row)
            ends.append(local_field[c, pl.ds((times - 1) * WIDE + row, 8), :])
            gains = [gain[j, pl.ds(row, 8), :] for j in range(chips)]
            added = combine(gains, ends) + offset[c, pl.ds(row, 8), :]
            if last:
                carry_in[c, pl.ds(row, 8), :] = added
            for t in range(times):
                value = local_field[c, pl.ds(t * WIDE + row, 8), :]
                value = value + power[pl.ds(t * WIDE + row, 8), :] * added
                at = pl.ds(t * TALL + 8 + row, 8)
                if last:
                    local_field[c, pl.ds(t * WIDE + row, 8), :] = value
                    value = value - field[c, at, :]
                field[c, at, :] = value

        over_planes(plane)

    def last_residual(c):
        def plane(x, row, parity):
            factors = factors_at(row)
            diagonal = 1.0 / scale[pl.ds(row, 8), :]
            for t in range(times):
                _, total = stencil(c, t, x, row, parity, factors)
                total = total * diagonal
                if t == 0:
                    added = carry_in[c, pl.ds(row, 8), :]
                    total = total - jnp.where(chip == 0, 2.0 * added, 0.0)
                source[c, pl.ds(t * CELLS + row, 8), :] = total

        over_planes(plane)

    def scatter(value, target, q):
        target[pl.ds(q, ROWS, stride=half), :] = value

    for q in range(half):
        slot = core * half + q
        scatter(viscosity[:, slot, :], scale, q)
        for d in range(3):
            scatter(peclet[d, :, slot, :], coefficient.at[2 * d], q)
        for c in range(COMPONENTS):
            scatter(initial[c, :, slot, :], start.at[c], q)
    for f in range(7):
        value = jnp.zeros((8, LANES), jnp.float32)
        for q in range(half):
            slot = core * half + q
            known = live[slot] > 0 if f == 6 else holder[slot, f] >= 0
            value = jnp.where(slot_index == q, jnp.where(known, 1.0, 0.0), value)
        present[f] = value

    def make(x, row, parity):
        at = pl.ds(row, 8)
        thickness = scale[at, :]
        inverse = 1.0 / (2.0 + 6.0 * thickness)
        scale[at, :] = inverse
        weight = thickness * inverse
        edges = [
            x == 0,
            x == PLANES - 1,
            (~y_upper) & first_block,
            y_upper & last_block,
            z_first,
            z_last,
        ]
        for d in range(3):
            number = coefficient[2 * d, at, :]
            for f, factor in ((2 * d, 1.0 + number), (2 * d + 1, 1.0 - number)):
                slot_edge = edges[f]
                value = weight * factor
                coefficient[f, at, :] = jnp.where(slot_edge, value * present[f], value)
        ratio = 2.0 * inverse
        total = ratio
        for t in range(times):
            power[pl.ds(t * WIDE + row, 8), :] = total
            if t == times - 1:
                for j, value in enumerate(gains_of(total)):
                    gain[j, at, :] = value
            total = total * ratio

    over_planes(make)
    ghost_y[...] = jnp.zeros_like(ghost_y)

    pack(power_message, lambda at: power[at, :], WIDE, 0)
    power_copies = copies(power_message, local_field, WIDE, 0, 0, carried=False)
    start_all(power_copies)

    def take(stage_ref, store):
        for origin in range(2):
            for j in range(local):
                for q in range(half):
                    store(origin * local + j, q, stage_ref[origin, q, :, j, :])

    for c in range(COMPONENTS):
        owns[c].wait()
        swaps[c].wait()

        def store(t, q, value, c=c):
            field[c, pl.ds(t * TALL + 8 + q, ROWS, stride=half), :] = value

        take(stage_iterate.at[:, :, c], store)
        pack(c, lambda at, c=c: field[c, at, :], TALL, 8)
        start_all(copies(c, field, TALL, 8, c))
    for c in range(COMPONENTS):
        owns[COMPONENTS + c].wait()
        swaps[COMPONENTS + c].wait()

        def store(t, q, value, c=c):
            force[c, pl.ds(t * CELLS + q, ROWS, stride=half), :] = value

        take(stage_forcing.at[:, :, c], store)

    wait_all(power_copies)
    for n in range(len(x_links)):
        for j, value in enumerate(gains_of(x_recv[power_message, n, pl.ds(4 * times, 4), :])):
            x_gain[n, j] = value
    for n in range(len(y_links)):
        for j, value in enumerate(gains_of(y_recv[power_message, n, pl.ds(32, 4), :])):
            y_gain[n, j] = value
    for side in range(2):
        ratio = z_recv[power_message, side, pl.ds(8 * (times - 1), 8), :]
        for j, value in enumerate(gains_of(ratio)):
            z_gain[side, j] = value

    def send_local(message, c):
        pack(message, lambda at: local_field[c, at, :], WIDE, 0)
        start_all(copies(message, local_field, WIDE, 0, c))

    def opening(c, carry):
        wait_all(copies(c, field, TALL, 8, c))
        ghosts(c, c, "raw")
        first_residual(c)
        send_local(COMPONENTS + c, c)
        first_offset(c, c)
        return carry

    lax.fori_loop(0, COMPONENTS, opening, 0)

    def turn(step, carry):
        c = lax.rem(step, COMPONENTS)
        message = COMPONENTS + step
        wait_all(copies(message, local_field, WIDE, 0, c))
        complete(message, c, False)
        ghosts(message, c, "next")
        sweep(c)
        send_local(message + COMPONENTS, c)
        return carry

    lax.fori_loop(0, COMPONENTS * (SWEEPS - 1), turn, 0)

    finals = []

    def give(c, stage_ref, load, out, number):
        for origin in range(2):
            for j in range(local):
                for q in range(half):
                    value = load(origin * local + j, q)
                    stage_ref[origin, q, c, :, j, :] = value(stage_ref[origin, q, c, :, j, :])
        other = 1 - core
        away = remote(
            stage_ref.at[other, :, c], out.at[mine, c], stage, number, peer
        )
        here = pltpu.make_async_copy(
            stage_ref.at[core, :, c], out.at[mine, c], stage_local.at[number]
        )
        away.start()
        here.start()
        finals.extend([away, here])

    for c in range(COMPONENTS):
        message = COMPONENTS * SWEEPS + c
        wait_all(copies(message, local_field, WIDE, 0, c))
        complete(message, c, True)

        def velocity(t, q, c=c):
            at = pl.ds(t * WIDE + q, ROWS, stride=half)
            return lambda held: held + local_field[c, at, :]

        give(c, stage_iterate, velocity, out_velocity, 2 * COMPONENTS + c)
        ghosts(message, c, "last")
        last_residual(c)

        def remainder(t, q, c=c):
            at = pl.ds(t * CELLS + q, ROWS, stride=half)
            return lambda held: source[c, at, :]

        give(c, stage_forcing, remainder, out_residual, 3 * COMPONENTS + c)
    for copy in finals:
        copy.wait()


def body(
    iterate,
    forcing,
    initial_velocity,
    viscosity,
    peclet,
    live_patch_mask,
    neighbour_holder,
    neighbour_slot,
):
    time_devices = lax.axis_size("tm")
    chips = time_devices // 2
    levels = lax.axis_size("space").bit_length() - 1
    slots, local = iterate.shape[:2]
    half = slots // 2
    times = 2 * local

    def by_rows(array):
        split = array.reshape(array.shape[:-1] + (ROWS, LANES))
        return split.transpose((0, 2, 3, 1, 4) if split.ndim == 5 else (1, 2, 0, 3))

    def whole(array):
        return array.transpose(0, 3, 1, 2, 4).reshape(slots, local, COMPONENTS, ROWS * LANES)

    count = [len(range(d, levels, 3)) for d in range(3)]
    messages = COMPONENTS * (SWEEPS + 1) + 1
    per_message = (chips - 1) + chips * (count[0] + count[1] + 1 + count[2])
    others = max(chips - 1, 1)
    f32 = jnp.float32
    stage = pltpu.VMEM((2, half, COMPONENTS, ROWS, local, LANES), f32)

    def rows(*shape):
        return pltpu.VMEM(shape + (LANES,), f32)

    nx, ny = max(count[0], 1), max(count[1], 1)
    x_rows, y_rows, z_rows = 4 * times + 8, 40, 8 * times
    result = jax.ShapeDtypeStruct((slots, COMPONENTS, ROWS, local, LANES), f32)
    velocity, residual = pl.pallas_call(
        functools.partial(kernel, (chips, levels, slots, local)),
        out_shape=(result, result),
        in_specs=[pl.BlockSpec(memory_space=pltpu.SMEM)] * 2
        + [pl.BlockSpec(memory_space=pl.ANY)] * 2
        + [pl.BlockSpec(memory_space=pltpu.VMEM)] * 3,
        out_specs=[pl.BlockSpec(memory_space=pl.ANY)] * 2,
        scratch_shapes=[
            stage,
            stage,
            rows(COMPONENTS, times * TALL),
            rows(COMPONENTS, times * WIDE),
            rows(COMPONENTS, times * CELLS),
            rows(COMPONENTS, times * CELLS),
            rows(COMPONENTS, CELLS),
            rows(COMPONENTS, times * WIDE),
            rows(COMPONENTS, times * 16),
            rows(6, CELLS),
            rows(times * WIDE),
            rows(CELLS),
            rows(chips, CELLS),
            rows(COMPONENTS, CELLS),
            rows(COMPONENTS, CELLS),
            rows(7, 8),
            rows(messages, nx, x_rows),
            rows(messages, nx, x_rows),
            rows(messages, ny, y_rows),
            rows(messages, ny, y_rows),
            rows(messages, 2, z_rows),
            rows(messages, 2, z_rows),
            rows(messages, nx, others, 8),
            rows(messages, ny, others, 8),
            rows(messages, 2, others, 8),
            rows(messages, others, CELLS),
            rows(nx, chips, 4),
            rows(ny, chips, 4),
            rows(2, chips, 8),
            rows(COMPONENTS, nx, 4),
            rows(COMPONENTS, ny, 4),
            rows(COMPONENTS, 2, 8),
            rows(COMPONENTS, nx, x_rows),
            rows(COMPONENTS, ny, y_rows),
            rows(COMPONENTS, 2, z_rows),
            pltpu.SemaphoreType.DMA((messages * per_message,)),
            pltpu.SemaphoreType.DMA((messages * per_message,)),
            pltpu.SemaphoreType.DMA((4 * COMPONENTS,)),
            pltpu.SemaphoreType.DMA((4 * COMPONENTS,)),
            pltpu.SemaphoreType.DMA((4 * COMPONENTS,)),
        ],
        compiler_params=pltpu.CompilerParams(
            collective_id=0, has_side_effects=True, vmem_limit_bytes=56 * 1024 * 1024
        ),
    )(
        neighbour_holder,
        live_patch_mask,
        by_rows(iterate),
        by_rows(forcing),
        by_rows(initial_velocity),
        viscosity.reshape(slots, ROWS, LANES).transpose(1, 0, 2),
        by_rows(peclet),
    )
    return whole(velocity), whole(residual)


def solution(mesh):
    return jax.shard_map(
        body,
        mesh=mesh,
        in_specs=(
            P("space", "tm", None, None),
            P("space", "tm", None, None),
            P("space", None, None),
            P("space", None),
            P("space", None, None),
            P("space"),
            P("space", None),
            P("space", None),
        ),
        out_specs=(P("space", "tm", None, None), P("space", "tm", None, None)),
        check_vma=False,
    )
```

time: 123 us -> 58.4 us (0.47)
  Pallas kernels: 112 us -> 53.6 us
  local copies, waits for them, and re-layouts: 8.37 us -> 3.97 us
  other arithmetic: 1.39 us -> 0 us
    pallas_call x1, Pallas kernels: 112 us -> 53.6 us  [body(): pl.pallas_call(functools.partial(kernel, (chips, levels, slots, local)),...]
    unnamed x7 -> x4, local copies, waits for them, and re-layouts: 7.38 us -> 3.97 us
where the time goes in v1:
time: 58.4 us; the launch traced here: 58.3 us
  Pallas kernels  53.6 us (92%)
  local copies, waits for them, and re-layouts  3.97 us (7%)
  between operations  0.65 us (1%)
    pallas_call x1, Pallas kernels, body(): pl.pallas_call(functools.partial(kernel, (chips, levels, slots, local)),...  53.6 us
    unnamed x4, local copies, waits for them, and re-layouts  3.97 us

profile of v1, /device:TPU:0, one launch (start us, length us, event | category | flops | bytes accessed | tf_op | source)
XLA Modules:
  0.0 58.3 jit_solution(12559232048811128699)
XLA Ops:
  0.6 53.6 %shard_map.86 = (f32[8,3,32,4,128]{4,3,2,1,0:T(4,128)}, f32[8,3,32,4,128]{4,3,2,1,0:T(4,128)}) custom-call(s32[8,6]{1,0:T(8,128)} %holder.1, s32[8]{0:T(128)} %live.1, f32[8,3,32,4,128]{4,3,2,1,0:T(4,128)} %bitcast.21, f32[8,3,32,4,128]{4,3,2,1,0:T(4,128)} %bitcast.22, f32[3,32,8,128]{3,2,1,0:T(8,128)} %bitcast.25, f32[32,8,128]{2,1,0:T(8,128)} %bitcast.27, ...), custom_call_target="tpu_custom_call" | custom-call | tf_op jit(solution)/shard_map/pallas_call | solution.py:676
  54.3 0.0 copy-start
  54.3 2.8 %copy.11 = f32[8,4,3,4096]{3,1,2,0:T(4,128)} copy(f32[8,4,3,4096]{3,1,2,0:T(4,128)} %bitcast.24) | data formatting | bytes 3145728
  57.1 0.0 copy-done
  57.1 1.1 %copy.12 = f32[8,4,3,4096]{3,1,2,0:T(4,128)} copy(f32[8,4,3,4096]{3,1,2,0:T(4,128)S(1)} %bitcast.23) | data formatting | bytes 3145728
Async XLA Ops:
  54.3 2.8 %copy-start = (f32[8,3,32,4,128]{4,3,2,1,0:T(4,128)S(1)}, f32[8,3,32,4,128]{4,3,2,1,0:T(4,128)}, u32[]{:S(2)}) copy-start(f32[8,3,32,4,128]{4,3,2,1,0:T(4,128)} %get-tuple-element.5) | copy-start | bytes 4718596

commit v2 on v1

--- a/solution.py
+++ b/solution.py
@@ -18,7 +18,7 @@
 CELLS = PLANES * 8
 TALL = CELLS + 24
 WIDE = CELLS + 8
-UNROLL = 4
+UNROLL = 8
 
 
 def kernel(
@@ -39,13 +39,17 @@
     source,
     force,
     start,
+    small_initial,
+    small_viscosity,
+    small_peclet,
     ghost_y,
     ghost_z,
     coefficient,
     power,
     scale,
     gain,
-    offset,
+    end_send,
+    carry,
     carry_in,
     present,
     x_send,
@@ -54,6 +58,8 @@
     y_recv,
     z_send,
     z_recv,
+    x_last,
+    y_last,
     x_end,
     y_end,
     z_end,
@@ -61,9 +67,6 @@
     x_gain,
     y_gain,
     z_gain,
-    x_offset,
-    y_offset,
-    z_offset,
     x_old,
     y_old,
     z_old,
@@ -72,6 +75,7 @@
     stage_send,
     stage_recv,
     stage_local,
+    small_sem,
 ):
     chips, levels, slots, local = dims
     half = slots // 2
@@ -123,7 +127,13 @@
     barrier = pltpu.get_barrier_semaphore()
     for target in greet:
         pl.semaphore_signal(barrier, inc=1, device_id=target, device_id_type=pl.DeviceIdType.MESH)
-    pl.semaphore_wait(barrier, len(greet))
+    smalls = [
+        pltpu.make_async_copy(viscosity, small_viscosity, small_sem.at[0]),
+        pltpu.make_async_copy(peclet, small_peclet, small_sem.at[1]),
+        pltpu.make_async_copy(initial, small_initial, small_sem.at[2]),
+    ]
+    for copy in smalls:
+        copy.start()
 
     def remote(src, dst, sems, number, device):
         return pltpu.make_async_remote_copy(
@@ -158,12 +168,15 @@
                 forcing.at[mine, c], stage_forcing.at[core, :, c], stage_local.at[COMPONENTS + c]
             )
         )
-    for copy in swaps + owns:
+    for copy in owns:
         copy.start()
+    pl.semaphore_wait(barrier, len(greet))
+    for copy in swaps:
+        copy.start()
 
     per_message = (chips - 1) + chips * (len(x_links) + len(y_links) + 1 + len(z_links))
 
-    def copies(message, buffer, pitch, base, c, carried=True):
+    def copies(message, c, ends=True):
         sems = (send_sem, recv_sem)
         number = [message * per_message]
         found = []
@@ -172,7 +185,33 @@
             found.append((remote(src, dst, sems, number[0], device), condition))
             number[0] = number[0] + 1
 
-        extra = range(1, chips) if carried else ()
+        last = pl.ds(8 * times, 8)
+        for j in range(1, chips) if ends else ():
+            for n, (side, partner) in enumerate(x_links):
+                add(
+                    x_last.at[message, n],
+                    x_end.at[message, n, j - 1],
+                    {"space": partner, "tm": seat(j, core)},
+                )
+            for n, (side, partner) in enumerate(y_links):
+                add(
+                    y_last.at[message, n],
+                    y_end.at[message, n, j - 1],
+                    {"space": partner, "tm": seat(j, core)},
+                )
+            for side, partner in z_links:
+                add(
+                    z_send.at[message, core, last],
+                    z_end.at[message, 1 - core, j - 1],
+                    {"space": partner, "tm": seat(j, 1 - core)},
+                    core == side,
+                )
+            add(
+                z_send.at[message, 1 - core, last],
+                z_end.at[message, core, j - 1],
+                {"tm": seat(j, 1 - core)},
+            )
+            add(end_send.at[c], end_recv.at[message, j - 1], {"tm": seat(j, core)})
         for n, (side, partner) in enumerate(x_links):
             add(x_send.at[message, n], x_recv.at[message, n], {"space": partner})
         for n, (side, partner) in enumerate(y_links):
@@ -185,34 +224,6 @@
                 core == side,
             )
         add(z_send.at[message, 1 - core], z_recv.at[message, core], peer)
-        for j in extra:
-            last = pl.ds((times - 1) * pitch + base, CELLS)
-            add(buffer.at[c, last], end_recv.at[message, j - 1], {"tm": seat(j, core)})
-            for n, (side, partner) in enumerate(x_links):
-                add(
-                    x_send.at[message, n, pl.ds(times * 4, 8)],
-                    x_end.at[message, n, j - 1],
-                    {"space": partner, "tm": seat(j, core)},
-                )
-            for n, (side, partner) in enumerate(y_links):
-                add(
-                    y_send.at[message, n, pl.ds(32, 8)],
-                    y_end.at[message, n, j - 1],
-                    {"space": partner, "tm": seat(j, core)},
-                )
-            end = pl.ds((times - 1) * 8, 8)
-            for side, partner in z_links:
-                add(
-                    z_send.at[message, core, end],
-                    z_end.at[message, 1 - core, j - 1],
-                    {"space": partner, "tm": seat(j, 1 - core)},
-                    core == side,
-                )
-            add(
-                z_send.at[message, 1 - core, end],
-                z_end.at[message, core, j - 1],
-                {"tm": seat(j, 1 - core)},
-            )
         return found
 
     def start_all(found):
@@ -233,13 +244,18 @@
         jnp.logical_or, [core == side for side, partner in z_links], jnp.bool_(False)
     )
 
-    def pack(message, load, pitch, base):
+    kept = jnp.where(chip == chips - 1, 0.0, 1.0)
+
+    def pack(message, load, pitch, base, first=None):
         for n, (side, partner) in enumerate(x_links):
             for t in range(times):
                 value = load(pl.ds(t * pitch + base + side * (CELLS - 7), 4, stride=2))
                 x_send[message, n, pl.ds(4 * t, 4), :] = value
+            if first is not None:
+                value = value + kept * x_send[first, n, pl.ds(4 * (times - 1), 4), :]
             x_send[message, n, pl.ds(4 * times, 4), :] = value
             x_send[message, n, pl.ds(4 * times + 4, 4), :] = value
+            x_last[message, n] = value
         for n, (side, partner) in enumerate(y_links):
             for k in range(4):
                 total = None
@@ -249,8 +265,12 @@
                     value = pltpu.roll(value, lax.rem(BLOCK_EDGE * i + 128 - 112 * side, 128), 1)
                     total = value if total is None else jnp.where(flat_lane == i, value, total)
                 y_send[message, n, pl.ds(8 * k, times), :] = total
-                y_send[message, n, pl.ds(32 + k, 1), :] = total[times - 1 : times]
-                y_send[message, n, pl.ds(36 + k, 1), :] = total[times - 1 : times]
+                ending = total[times - 1 : times]
+                if first is not None:
+                    ending = ending + kept * y_send[first, n, pl.ds(8 * k + times - 1, 1), :]
+                y_send[message, n, pl.ds(32 + k, 1), :] = ending
+                y_send[message, n, pl.ds(36 + k, 1), :] = ending
+                y_last[message, n, pl.ds(k, 1), :] = ending
         for t in range(times):
             low = high = None
             for x in range(PLANES):
@@ -258,15 +278,16 @@
                 value = pltpu.roll(value, (x - 15) % 128, 1)
                 high = value if high is None else jnp.where(z_index == x, value, high)
                 low = value if low is None else jnp.where(z_index == (x + 1) % 16, value, low)
-            z_send[message, 1, pl.ds(8 * t, 8), :] = high
-            z_send[message, 0, pl.ds(8 * t, 8), :] = pltpu.roll(low, 15, 1)
+            pair = (pltpu.roll(low, 15, 1), high)
+            for side in range(2):
+                z_send[message, side, pl.ds(8 * t, 8), :] = pair[side]
+                if t == times - 1:
+                    value = pair[side]
+                    if first is not None:
+                        value = value + kept * z_send[first, side, pl.ds(8 * t, 8), :]
+                    z_send[message, side, pl.ds(8 * times, 8), :] = value
 
     wraps = [jnp.where(chip - j < 0, ALPHA_SCALE, 1.0) for j in range(1, chips + 1)]
-    keeps = [
-        jnp.where(lax.rem(chip - j + chips, chips) == chips - 1, 0.0, 1.0)
-        for j in range(1, chips + 1)
-    ]
-
     def gains_of(ratio):
         powers = [jnp.ones_like(ratio)]
         for j in range(chips):
@@ -274,26 +295,23 @@
         scaled = 1.0 / (1.0 - ALPHA_SCALE * powers[chips])
         return [wraps[j] * (powers[j] * scaled) for j in range(chips)]
 
-    def combine(gains, ends, weights=None):
-        total = None
-        for j in range(chips):
-            term = gains[j] * ends[j]
-            if weights is not None:
-                term = term * weights[j]
-            total = term if total is None else total + term
+    def combine(gains, ends):
+        total = gains[0] * ends[0]
+        for j in range(1, chips):
+            total = total + gains[j] * ends[j]
         return total
 
     def x_ends(message, n):
-        found = [x_end[message, n, j, pl.ds(0, 4), :] for j in range(chips - 1)]
+        found = [x_end[message, n, j] for j in range(chips - 1)]
         return found + [x_recv[message, n, pl.ds(4 * times, 4), :]]
 
     def y_ends(message, n):
-        found = [y_end[message, n, j, pl.ds(0, 4), :] for j in range(chips - 1)]
+        found = [y_end[message, n, j] for j in range(chips - 1)]
         return found + [y_recv[message, n, pl.ds(32, 4), :]]
 
     def z_ends(message, side):
         found = [z_end[message, side, j] for j in range(chips - 1)]
-        return found + [z_recv[message, side, pl.ds(8 * (times - 1), 8), :]]
+        return found + [z_recv[message, side, pl.ds(8 * times, 8), :]]
 
     def ghosts(message, c, mode):
         def finish(value, old, index):
@@ -309,13 +327,8 @@
             field[c, pl.ds(base, 8), :] = field[c, pl.ds(base + CELLS - 1, 8), :]
             field[c, pl.ds(base + CELLS + 8, 8), :] = field[c, pl.ds(base + 9, 8), :]
         for n, (side, partner) in enumerate(x_links):
-            if mode == "raw":
-                x_offset[c, n] = combine(
-                    [x_gain[n, j] for j in range(chips)], x_ends(message, n), keeps
-                )
-            else:
+            if mode != "raw":
                 added = combine([x_gain[n, j] for j in range(chips)], x_ends(message, n))
-                added = added + x_offset[c, n]
             for t in range(times):
                 at = pl.ds(4 * t, 4)
                 value = x_recv[message, n, at, :]
@@ -324,13 +337,8 @@
                 value = finish(value, x_old, (c, n, at, slice(None)))
                 field[c, pl.ds(t * TALL + side * (CELLS + 9), 4, stride=2), :] = value
         for n, (side, partner) in enumerate(y_links):
-            if mode == "raw":
-                y_offset[c, n] = combine(
-                    [y_gain[n, j] for j in range(chips)], y_ends(message, n), keeps
-                )
-            else:
+            if mode != "raw":
                 added = combine([y_gain[n, j] for j in range(chips)], y_ends(message, n))
-                added = added + y_offset[c, n]
             for k in range(4):
                 at = pl.ds(8 * k, times)
                 value = y_recv[message, n, at, :]
@@ -345,12 +353,9 @@
                     ghost_y[c, pl.ds(row, times, stride=WIDE), :] = turned
         added = [None, None]
         for side in range(2):
-            ends = z_ends(message, side)
-            gains = [z_gain[side, j] for j in range(chips)]
-            if mode == "raw":
-                z_offset[c, side] = combine(gains, ends, keeps)
-            else:
-                added[side] = combine(gains, ends) + z_offset[c, side]
+            if mode != "raw":
+                gains = [z_gain[side, j] for j in range(chips)]
+                added[side] = combine(gains, z_ends(message, side))
         even = z_index % 2 == 0
         for t in range(times):
             at = pl.ds(8 * t, 8)
@@ -409,6 +414,7 @@
                     total = total + ratio * before
                 local_field[c, pl.ds(t * WIDE + row, 8), :] = total
                 before = total
+            end_send[c, pl.ds(row, 8), :] = before + carry[c, pl.ds(row, 8), :]
 
         over_planes(plane)
 
@@ -429,28 +435,18 @@
                     total = total + ratio * before
                 local_field[c, pl.ds(t * WIDE + row, 8), :] = total
                 before, earlier = total, value
-
-        over_planes(plane)
-
-    def own_ends(message, c, row):
-        found = [end_recv[message, j, pl.ds(row, 8), :] for j in range(chips - 1)]
-        return found
-
-    def first_offset(message, c):
-        def plane(x, row, parity):
-            ends = own_ends(message, c, row)
-            ends.append(field[c, pl.ds((times - 1) * TALL + 8 + row, 8), :])
-            gains = [gain[j, pl.ds(row, 8), :] for j in range(chips)]
-            offset[c, pl.ds(row, 8), :] = combine(gains, ends, keeps) * present[6]
+            kept_end = kept * (earlier * alive)
+            carry[c, pl.ds(row, 8), :] = kept_end
+            end_send[c, pl.ds(row, 8), :] = before + kept_end
 
         over_planes(plane)
 
     def complete(message, c, last):
         def plane(x, row, parity):
-            ends = own_ends(message, c, row)
-            ends.append(local_field[c, pl.ds((times - 1) * WIDE + row, 8), :])
+            ends = [end_recv[message, j, pl.ds(row, 8), :] for j in range(chips - 1)]
+            ends.append(end_send[c, pl.ds(row, 8), :])
             gains = [gain[j, pl.ds(row, 8), :] for j in range(chips)]
-            added = combine(gains, ends) + offset[c, pl.ds(row, 8), :]
+            added = combine(gains, ends)
             if last:
                 carry_in[c, pl.ds(row, 8), :] = added
             for t in range(times):
@@ -481,13 +477,15 @@
     def scatter(value, target, q):
         target[pl.ds(q, ROWS, stride=half), :] = value
 
+    for copy in smalls:
+        copy.wait()
     for q in range(half):
         slot = core * half + q
-        scatter(viscosity[:, slot, :], scale, q)
+        scatter(small_viscosity[:, slot, :], scale, q)
         for d in range(3):
-            scatter(peclet[d, :, slot, :], coefficient.at[2 * d], q)
+            scatter(small_peclet[d, :, slot, :], coefficient.at[2 * d], q)
         for c in range(COMPONENTS):
-            scatter(initial[c, :, slot, :], start.at[c], q)
+            scatter(small_initial[c, :, slot, :], start.at[c], q)
     for f in range(7):
         value = jnp.zeros((8, LANES), jnp.float32)
         for q in range(half):
@@ -529,14 +527,14 @@
     ghost_y[...] = jnp.zeros_like(ghost_y)
 
     pack(power_message, lambda at: power[at, :], WIDE, 0)
-    power_copies = copies(power_message, local_field, WIDE, 0, 0, carried=False)
+    power_copies = copies(power_message, 0, ends=False)
     start_all(power_copies)
 
     def take(stage_ref, store):
         for origin in range(2):
             for j in range(local):
                 for q in range(half):
-                    store(origin * local + j, q, stage_ref[origin, q, :, j, :])
+                    store(origin * local + j, q, stage_ref[origin, q, pl.ds(j, ROWS, stride=local), :])
 
     for c in range(COMPONENTS):
         owns[c].wait()
@@ -547,7 +545,7 @@
 
         take(stage_iterate.at[:, :, c], store)
         pack(c, lambda at, c=c: field[c, at, :], TALL, 8)
-        start_all(copies(c, field, TALL, 8, c))
+        start_all(copies(c, c, ends=False))
     for c in range(COMPONENTS):
         owns[COMPONENTS + c].wait()
         swaps[COMPONENTS + c].wait()
@@ -565,20 +563,19 @@
         for j, value in enumerate(gains_of(y_recv[power_message, n, pl.ds(32, 4), :])):
             y_gain[n, j] = value
     for side in range(2):
-        ratio = z_recv[power_message, side, pl.ds(8 * (times - 1), 8), :]
+        ratio = z_recv[power_message, side, pl.ds(8 * times, 8), :]
         for j, value in enumerate(gains_of(ratio)):
             z_gain[side, j] = value
 
     def send_local(message, c):
-        pack(message, lambda at: local_field[c, at, :], WIDE, 0)
-        start_all(copies(message, local_field, WIDE, 0, c))
+        pack(message, lambda at: local_field[c, at, :], WIDE, 0, c)
+        start_all(copies(message, c))
 
     def opening(c, carry):
-        wait_all(copies(c, field, TALL, 8, c))
+        wait_all(copies(c, c, ends=False))
         ghosts(c, c, "raw")
         first_residual(c)
         send_local(COMPONENTS + c, c)
-        first_offset(c, c)
         return carry
 
     lax.fori_loop(0, COMPONENTS, opening, 0)
@@ -586,7 +583,7 @@
     def turn(step, carry):
         c = lax.rem(step, COMPONENTS)
         message = COMPONENTS + step
-        wait_all(copies(message, local_field, WIDE, 0, c))
+        wait_all(copies(message, c))
         complete(message, c, False)
         ghosts(message, c, "next")
         sweep(c)
@@ -602,7 +599,8 @@
             for j in range(local):
                 for q in range(half):
                     value = load(origin * local + j, q)
-                    stage_ref[origin, q, c, :, j, :] = value(stage_ref[origin, q, c, :, j, :])
+                    at = pl.ds(j, ROWS, stride=local)
+                    stage_ref[origin, q, c, at, :] = value(stage_ref[origin, q, c, at, :])
         other = 1 - core
         away = remote(
             stage_ref.at[other, :, c], out.at[mine, c], stage, number, peer
@@ -616,7 +614,7 @@
 
     for c in range(COMPONENTS):
         message = COMPONENTS * SWEEPS + c
-        wait_all(copies(message, local_field, WIDE, 0, c))
+        wait_all(copies(message, c))
         complete(message, c, True)
 
         def velocity(t, q, c=c):
@@ -655,30 +653,33 @@
 
     def by_rows(array):
         split = array.reshape(array.shape[:-1] + (ROWS, LANES))
-        return split.transpose((0, 2, 3, 1, 4) if split.ndim == 5 else (1, 2, 0, 3))
+        if split.ndim == 4:
+            return split.transpose(1, 2, 0, 3)
+        split = split.transpose(0, 2, 3, 1, 4)
+        return split.reshape(slots, COMPONENTS, ROWS * local, LANES)
 
     def whole(array):
-        return array.transpose(0, 3, 1, 2, 4).reshape(slots, local, COMPONENTS, ROWS * LANES)
+        split = array.reshape(slots, COMPONENTS, ROWS, local, LANES)
+        return split.transpose(0, 3, 1, 2, 4).reshape(slots, local, COMPONENTS, ROWS * LANES)
 
     count = [len(range(d, levels, 3)) for d in range(3)]
     messages = COMPONENTS * (SWEEPS + 1) + 1
     per_message = (chips - 1) + chips * (count[0] + count[1] + 1 + count[2])
     others = max(chips - 1, 1)
     f32 = jnp.float32
-    stage = pltpu.VMEM((2, half, COMPONENTS, ROWS, local, LANES), f32)
+    stage = pltpu.VMEM((2, half, COMPONENTS, ROWS * local, LANES), f32)
 
     def rows(*shape):
         return pltpu.VMEM(shape + (LANES,), f32)
 
     nx, ny = max(count[0], 1), max(count[1], 1)
-    x_rows, y_rows, z_rows = 4 * times + 8, 40, 8 * times
-    result = jax.ShapeDtypeStruct((slots, COMPONENTS, ROWS, local, LANES), f32)
+    x_rows, y_rows, z_rows = 4 * times + 8, 40, 8 * times + 8
+    result = jax.ShapeDtypeStruct((slots, COMPONENTS, ROWS * local, LANES), f32)
     velocity, residual = pl.pallas_call(
         functools.partial(kernel, (chips, levels, slots, local)),
         out_shape=(result, result),
         in_specs=[pl.BlockSpec(memory_space=pltpu.SMEM)] * 2
-        + [pl.BlockSpec(memory_space=pl.ANY)] * 2
-        + [pl.BlockSpec(memory_space=pltpu.VMEM)] * 3,
+        + [pl.BlockSpec(memory_space=pl.ANY)] * 5,
         out_specs=[pl.BlockSpec(memory_space=pl.ANY)] * 2,
         scratch_shapes=[
             stage,
@@ -688,12 +689,16 @@
             rows(COMPONENTS, times * CELLS),
             rows(COMPONENTS, times * CELLS),
             rows(COMPONENTS, CELLS),
+            rows(COMPONENTS, ROWS, slots),
+            rows(ROWS, slots),
+            rows(COMPONENTS, ROWS, slots),
             rows(COMPONENTS, times * WIDE),
             rows(COMPONENTS, times * 16),
             rows(6, CELLS),
             rows(times * WIDE),
             rows(CELLS),
             rows(chips, CELLS),
+            rows(COMPONENTS, CELLS),
             rows(COMPONENTS, CELLS),
             rows(COMPONENTS, CELLS),
             rows(7, 8),
@@ -703,16 +708,15 @@
             rows(messages, ny, y_rows),
             rows(messages, 2, z_rows),
             rows(messages, 2, z_rows),
-            rows(messages, nx, others, 8),
-            rows(messages, ny, others, 8),
+            rows(messages, nx, 4),
+            rows(messages, ny, 4),
+            rows(messages, nx, others, 4),
+            rows(messages, ny, others, 4),
             rows(messages, 2, others, 8),
             rows(messages, others, CELLS),
             rows(nx, chips, 4),
             rows(ny, chips, 4),
             rows(2, chips, 8),
-            rows(COMPONENTS, nx, 4),
-            rows(COMPONENTS, ny, 4),
-            rows(COMPONENTS, 2, 8),
             rows(COMPONENTS, nx, x_rows),
             rows(COMPONENTS, ny, y_rows),
             rows(COMPONENTS, 2, z_rows),
@@ -721,6 +725,7 @@
             pltpu.SemaphoreType.DMA((4 * COMPONENTS,)),
             pltpu.SemaphoreType.DMA((4 * COMPONENTS,)),
             pltpu.SemaphoreType.DMA((4 * COMPONENTS,)),
+            pltpu.SemaphoreType.DMA((3,)),
         ],
         compiler_params=pltpu.CompilerParams(
             collective_id=0, has_side_effects=True, vmem_limit_bytes=56 * 1024 * 1024

time: 58.4 us -> 51.9 us (0.89)
  Pallas kernels: 53.6 us -> 47.1 us
    pallas_call x1, Pallas kernels: 53.6 us -> 47.1 us  [body(): pl.pallas_call(functools.partial(kernel, (chips, levels, slots, local)),...]
where the time goes in v2:
time: 51.9 us; the launch traced here: 51.8 us
  Pallas kernels  47.1 us (91%)
  local copies, waits for them, and re-layouts  3.97 us (8%)
  between operations  0.65 us (1%)
    pallas_call x1, Pallas kernels, body(): pl.pallas_call(functools.partial(kernel, (chips, levels, slots, local)),...  47.1 us
    unnamed x4, local copies, waits for them, and re-layouts  3.97 us

profile of v2, /device:TPU:0, one launch (start us, length us, event | category | flops | bytes accessed | tf_op | source)
XLA Modules:
  0.0 51.8 jit_solution(13110313122455435378)
XLA Ops:
  0.6 47.1 %shard_map.86 = (f32[8,3,128,128]{3,2,1,0:T(8,128)}, f32[8,3,128,128]{3,2,1,0:T(8,128)}) custom-call(s32[8,6]{1,0:T(8,128)} %holder.1, s32[8]{0:T(128)} %live.1, f32[8,3,128,128]{3,2,1,0:T(8,128)} %bitcast.29, f32[8,3,128,128]{3,2,1,0:T(8,128)} %bitcast.30, f32[3,32,8,128]{3,2,1,0:T(8,128)} %bitcast.33, f32[32,8,128]{2,1,0:T(8,128)} %bitcast.35, ...), custom_call_target="tpu_custom_call" | custom-call | tf_op jit(solution)/shard_map/pallas_call | solution.py:678
  47.8 0.0 copy-start
  47.8 2.8 %copy.15 = f32[8,4,3,4096]{3,1,2,0:T(4,128)} copy(f32[8,4,3,4096]{3,1,2,0:T(4,128)} %bitcast.32) | data formatting | bytes 3145728
  50.6 0.0 copy-done
  50.6 1.1 %copy.16 = f32[8,4,3,4096]{3,1,2,0:T(4,128)} copy(f32[8,4,3,4096]{3,1,2,0:T(4,128)S(1)} %bitcast.31) | data formatting | bytes 3145728
Async XLA Ops:
  47.8 2.8 %copy-start = (f32[8,3,128,128]{3,2,1,0:T(8,128)S(1)}, f32[8,3,128,128]{3,2,1,0:T(8,128)}, u32[]{:S(2)}) copy-start(f32[8,3,128,128]{3,2,1,0:T(8,128)} %get-tuple-element.5) | copy-start | bytes 4718596

commit v3 on v2

--- a/solution.py
+++ b/solution.py
@@ -18,7 +18,7 @@
 CELLS = PLANES * 8
 TALL = CELLS + 24
 WIDE = CELLS + 8
-UNROLL = 8
+UNROLL = 16
 
 
 def kernel(
@@ -176,7 +176,7 @@
 
     per_message = (chips - 1) + chips * (len(x_links) + len(y_links) + 1 + len(z_links))
 
-    def copies(message, c, ends=True):
+    def copies(message, ends=True):
         sems = (send_sem, recv_sem)
         number = [message * per_message]
         found = []
@@ -186,6 +186,7 @@
             number[0] = number[0] + 1
 
         last = pl.ds(8 * times, 8)
+        number[0] = number[0] + chips - 1
         for j in range(1, chips) if ends else ():
             for n, (side, partner) in enumerate(x_links):
                 add(
@@ -211,7 +212,6 @@
                 z_end.at[message, core, j - 1],
                 {"tm": seat(j, 1 - core)},
             )
-            add(end_send.at[c], end_recv.at[message, j - 1], {"tm": seat(j, core)})
         for n, (side, partner) in enumerate(x_links):
             add(x_send.at[message, n], x_recv.at[message, n], {"space": partner})
         for n, (side, partner) in enumerate(y_links):
@@ -225,6 +225,21 @@
             )
         add(z_send.at[message, 1 - core], z_recv.at[message, core], peer)
         return found
+
+    def carries(message, c):
+        return [
+            (
+                remote(
+                    end_send.at[c],
+                    end_recv.at[message, j - 1],
+                    (send_sem, recv_sem),
+                    message * per_message + j - 1,
+                    {"tm": seat(j, core)},
+                ),
+                None,
+            )
+            for j in range(1, chips)
+        ]
 
     def start_all(found):
         for copy, condition in found:
@@ -527,7 +542,7 @@
     ghost_y[...] = jnp.zeros_like(ghost_y)
 
     pack(power_message, lambda at: power[at, :], WIDE, 0)
-    power_copies = copies(power_message, 0, ends=False)
+    power_copies = copies(power_message, ends=False)
     start_all(power_copies)
 
     def take(stage_ref, store):
@@ -545,7 +560,7 @@
 
         take(stage_iterate.at[:, :, c], store)
         pack(c, lambda at, c=c: field[c, at, :], TALL, 8)
-        start_all(copies(c, c, ends=False))
+        start_all(copies(c, ends=False))
     for c in range(COMPONENTS):
         owns[COMPONENTS + c].wait()
         swaps[COMPONENTS + c].wait()
@@ -569,10 +584,11 @@
 
     def send_local(message, c):
         pack(message, lambda at: local_field[c, at, :], WIDE, 0, c)
-        start_all(copies(message, c))
+        start_all(copies(message))
+        start_all(carries(message, c))
 
     def opening(c, carry):
-        wait_all(copies(c, c, ends=False))
+        wait_all(copies(c, ends=False))
         ghosts(c, c, "raw")
         first_residual(c)
         send_local(COMPONENTS + c, c)
@@ -583,7 +599,8 @@
     def turn(step, carry):
         c = lax.rem(step, COMPONENTS)
         message = COMPONENTS + step
-        wait_all(copies(message, c))
+        wait_all(copies(message))
+        wait_all(carries(message, c))
         complete(message, c, False)
         ghosts(message, c, "next")
         sweep(c)
@@ -600,10 +617,10 @@
                 for q in range(half):
                     value = load(origin * local + j, q)
                     at = pl.ds(j, ROWS, stride=local)
-                    stage_ref[origin, q, c, at, :] = value(stage_ref[origin, q, c, at, :])
-        other = 1 - core
+                    value = value(stage_ref[origin, q, c, at, :])
+                    stage_ref[origin, q, c, at, :] = value
         away = remote(
-            stage_ref.at[other, :, c], out.at[mine, c], stage, number, peer
+            stage_ref.at[1 - core, :, c], out.at[mine, c], stage, number, peer
         )
         here = pltpu.make_async_copy(
             stage_ref.at[core, :, c], out.at[mine, c], stage_local.at[number]
@@ -614,7 +631,7 @@
 
     for c in range(COMPONENTS):
         message = COMPONENTS * SWEEPS + c
-        wait_all(copies(message, c))
+        wait_all(carries(message, c))
         complete(message, c, True)
 
         def velocity(t, q, c=c):
@@ -622,6 +639,7 @@
             return lambda held: held + local_field[c, at, :]
 
         give(c, stage_iterate, velocity, out_velocity, 2 * COMPONENTS + c)
+        wait_all(copies(message))
         ghosts(message, c, "last")
         last_residual(c)
 
@@ -631,6 +649,17 @@
 
         give(c, stage_forcing, remainder, out_residual, 3 * COMPONENTS + c)
     for copy in finals:
+        copy.wait()
+
+
+def emit(first, second, first_out, second_out, sem):
+    copies = [
+        pltpu.make_async_copy(first, first_out, sem.at[0]),
+        pltpu.make_async_copy(second, second_out, sem.at[1]),
+    ]
+    for copy in copies:
+        copy.start()
+    for copy in copies:
         copy.wait()
 
 
@@ -674,7 +703,7 @@
 
     nx, ny = max(count[0], 1), max(count[1], 1)
     x_rows, y_rows, z_rows = 4 * times + 8, 40, 8 * times + 8
-    result = jax.ShapeDtypeStruct((slots, COMPONENTS, ROWS * local, LANES), f32)
+    result = pltpu.VMEM((slots, COMPONENTS, ROWS * local, LANES), f32)
     velocity, residual = pl.pallas_call(
         functools.partial(kernel, (chips, levels, slots, local)),
         out_shape=(result, result),
@@ -728,7 +757,7 @@
             pltpu.SemaphoreType.DMA((3,)),
         ],
         compiler_params=pltpu.CompilerParams(
-            collective_id=0, has_side_effects=True, vmem_limit_bytes=56 * 1024 * 1024
+            collective_id=0, has_side_effects=True, vmem_limit_bytes=121 * 512 * 1024
         ),
     )(
         neighbour_holder,
@@ -739,6 +768,17 @@
         viscosity.reshape(slots, ROWS, LANES).transpose(1, 0, 2),
         by_rows(peclet),
     )
+    shape = jax.ShapeDtypeStruct((slots, COMPONENTS, ROWS * local, LANES), f32)
+    velocity = pltpu.with_memory_space_constraint(velocity, pltpu.MemorySpace.VMEM)
+    residual = pltpu.with_memory_space_constraint(residual, pltpu.MemorySpace.VMEM)
+    velocity, residual = pl.pallas_call(
+        emit,
+        out_shape=(shape, shape),
+        in_specs=[pl.BlockSpec(memory_space=pltpu.MemorySpace.VMEM)] * 2,
+        out_specs=[pl.BlockSpec(memory_space=pl.ANY)] * 2,
+        scratch_shapes=[pltpu.SemaphoreType.DMA((2,))],
+        compiler_params=pltpu.CompilerParams(vmem_limit_bytes=4 * 1024 * 1024),
+    )(velocity, residual)
     return whole(velocity), whole(residual)
 
 

time: 51.9 us -> 48.7 us (0.938)
  local copies, waits for them, and re-layouts: 3.97 us -> 0 us
  Pallas kernels: 47.1 us -> 47.9 us
    unnamed x4 -> x0, local copies, waits for them, and re-layouts: 3.97 us -> none
    pallas_call x0 -> x1, Pallas kernels: none -> 1.68 us  [body(): pl.pallas_call(emit, out_shape=(shape, shape), in_specs=[pl.BlockSpec(mem...]
    pallas_call x1, Pallas kernels: 47.1 us -> 46.2 us  [body(): pl.pallas_call(functools.partial(kernel, (chips, levels, slots, local)),...]
where the time goes in v3:
time: 48.7 us; the launch traced here: 48.6 us
  Pallas kernels  47.9 us (98%)
  between operations  0.64 us (1%)
    pallas_call x1, Pallas kernels, body(): pl.pallas_call(functools.partial(kernel, (chips, levels, slots, local)),...  46.2 us
    pallas_call x1, Pallas kernels, body(): pl.pallas_call(emit, out_shape=(shape, shape), in_specs=[pl.BlockSpec(mem...  1.68 us

profile of v3, /device:TPU:0, one launch (start us, length us, event | category | flops | bytes accessed | tf_op | source)
XLA Modules:
  0.0 48.6 jit_solution(4877785820188404507)
XLA Ops:
  0.6 46.2 %shard_map.86 = (f32[8,3,128,128]{3,2,1,0:T(8,128)S(1)}, f32[8,3,128,128]{3,2,1,0:T(8,128)S(1)}) custom-call(s32[8,6]{1,0:T(8,128)} %holder.1, s32[8]{0:T(128)} %live.1, f32[8,3,128,128]{3,2,1,0:T(8,128)} %bitcast.29, f32[8,3,128,128]{3,2,1,0:T(8,128)} %bitcast.30, f32[3,32,8,128]{3,2,1,0:T(8,128)} %bitcast.31, f32[32,8,128]{2,1,0:T(8,128)} %bitcast.33, ...), custom_call_target="tpu_custom_call" | custom-call | tf_op jit(solution)/shard_map/pallas_call | solution.py:707
  46.9 1.7 %shard_map.87 = (f32[8,3,128,128]{3,2,1,0:T(8,128)}, f32[8,3,128,128]{3,2,1,0:T(8,128)}) custom-call(f32[8,3,128,128]{3,2,1,0:T(8,128)S(1)} %get-tuple-element.6.first, f32[8,3,128,128]{3,2,1,0:T(8,128)S(1)} %get-tuple-element.7.second), custom_call_target="tpu_custom_call" | custom-call | tf_op jit(solution)/shard_map/pallas_call | solution.py:774

commit v4 on v3

--- a/solution.py
+++ b/solution.py
@@ -34,6 +34,7 @@
     out_residual,
     stage_iterate,
     stage_forcing,
+    stage_away,
     field,
     local_field,
     source,
@@ -60,6 +61,8 @@
     z_recv,
     x_last,
     y_last,
+    y_first_send,
+    y_first_recv,
     x_end,
     y_end,
     z_end,
@@ -75,6 +78,7 @@
     stage_send,
     stage_recv,
     stage_local,
+    away_sem,
     small_sem,
 ):
     chips, levels, slots, local = dims
@@ -121,9 +125,11 @@
     greet = [{"tm": seat(j, core)} for j in range(1, chips)]
     for side, partner in x_links + y_links:
         greet += [{"space": partner, "tm": seat(j, core)} for j in range(chips)]
+        greet.append({"space": partner, "tm": seat(0, 1 - core)})
     greet += [{"tm": seat(j, 1 - core)} for j in range(chips)]
     for side, partner in z_links:
         greet += [{"space": partner, "tm": seat(j, 1 - core)} for j in range(chips)]
+        greet.append({"space": partner})
     barrier = pltpu.get_barrier_semaphore()
     for target in greet:
         pl.semaphore_signal(barrier, inc=1, device_id=target, device_id_type=pl.DeviceIdType.MESH)
@@ -149,7 +155,7 @@
     mine = pl.ds(core * half, half)
     theirs = pl.ds((1 - core) * half, half)
     stage = (stage_send, stage_recv)
-    swaps, owns = [], []
+    swaps, owns, aways = [], [], []
     for c in range(COMPONENTS):
         swaps.append(
             remote(iterate.at[theirs, c], stage_iterate.at[core, :, c], stage, c, peer)
@@ -159,35 +165,41 @@
                 iterate.at[mine, c], stage_iterate.at[core, :, c], stage_local.at[c]
             )
         )
-    for c in range(COMPONENTS):
+        aways.append(
+            pltpu.make_async_copy(iterate.at[theirs, c], stage_away.at[:, c], away_sem.at[c])
+        )
         swaps.append(
             remote(forcing.at[theirs, c], stage_forcing.at[core, :, c], stage, COMPONENTS + c, peer)
         )
+    for c in range(COMPONENTS):
         owns.append(
             pltpu.make_async_copy(
                 forcing.at[mine, c], stage_forcing.at[core, :, c], stage_local.at[COMPONENTS + c]
             )
         )
-    for copy in owns:
+    for c in range(COMPONENTS):
+        owns[c].start()
+        aways[c].start()
+    for copy in owns[COMPONENTS:]:
         copy.start()
-    pl.semaphore_wait(barrier, len(greet))
-    for copy in swaps:
-        copy.start()
 
     per_message = (chips - 1) + chips * (len(x_links) + len(y_links) + 1 + len(z_links))
 
-    def copies(message, ends=True):
+    def collector(message, start):
         sems = (send_sem, recv_sem)
-        number = [message * per_message]
+        number = [message * per_message + start]
         found = []
 
         def add(src, dst, device, condition=None):
             found.append((remote(src, dst, sems, number[0], device), condition))
             number[0] = number[0] + 1
 
+        return found, add
+
+    def faces(message):
+        found, add = collector(message, chips - 1)
         last = pl.ds(8 * times, 8)
-        number[0] = number[0] + chips - 1
-        for j in range(1, chips) if ends else ():
+        for j in range(1, chips):
             for n, (side, partner) in enumerate(x_links):
                 add(
                     x_last.at[message, n],
@@ -212,6 +224,10 @@
                 z_end.at[message, core, j - 1],
                 {"tm": seat(j, 1 - core)},
             )
+        return found
+
+    def halos(message):
+        found, add = collector(message, per_message - per_message // chips)
         for n, (side, partner) in enumerate(x_links):
             add(x_send.at[message, n], x_recv.at[message, n], {"space": partner})
         for n, (side, partner) in enumerate(y_links):
@@ -225,6 +241,90 @@
             )
         add(z_send.at[message, 1 - core], z_recv.at[message, core], peer)
         return found
+
+    def first_copies(c):
+        sems = (send_sem, recv_sem)
+        number = [c * per_message]
+        both, sent, arrived = [], [], []
+
+        def take_number():
+            number[0] = number[0] + 1
+            return number[0] - 1
+
+        x_size, z_size = 4 * local, 8 * local
+
+        def piece(which, size):
+            return pl.ds(pl.multiple_of(which * size, size), size)
+
+        for group in (core, 1 - core):
+            for n, (side, partner) in enumerate(x_links):
+                both.append(
+                    remote(
+                        x_send.at[c, n, piece(group, x_size)],
+                        x_recv.at[c, n, piece(core, x_size)],
+                        sems,
+                        take_number(),
+                        {"space": partner, "tm": seat(0, group)},
+                    )
+                )
+            for n, (side, partner) in enumerate(y_links):
+                both.append(
+                    remote(
+                        y_first_send.at[c, n, group],
+                        y_first_recv.at[c, n, core],
+                        sems,
+                        take_number(),
+                        {"space": partner, "tm": seat(0, group)},
+                    )
+                )
+        for side, partner in z_links:
+            numbers = [take_number(), take_number()]
+
+            def outer(index, side=side, partner=partner):
+                return remote(
+                    z_send.at[c, side, piece(side, z_size)],
+                    z_recv.at[c, 1 - side, piece(core, z_size)],
+                    sems,
+                    index,
+                    {"space": partner, "tm": seat(0, 1 - side)},
+                )
+
+            sent.append(outer(numbers[0] + core))
+            for index in numbers:
+                arrived.append((outer(index), core == side))
+        both.append(
+            remote(
+                z_send.at[c, 1 - core, piece(core, z_size)],
+                z_recv.at[c, core, piece(core, z_size)],
+                sems,
+                take_number(),
+                peer,
+            )
+        )
+        return both, sent, arrived
+
+    def start_first(c):
+        both, sent, arrived = first_copies(c)
+        for copy in both + sent:
+            copy.start()
+
+    def wait_first(c):
+        both, sent, arrived = first_copies(c)
+        for copy in both:
+            copy.wait()
+        for copy in sent:
+            copy.wait_send()
+        for copy, condition in arrived:
+            pl.when(condition)(copy.wait_recv)
+        for j in range(local):
+            source_row = pl.ds(8 * ((1 - core) * local + j), 8)
+            target_row = pl.ds(8 * (core * local + j), 8)
+            z_recv[c, 1 - core, target_row, :] = z_send[c, core, source_row, :]
+        for n in range(len(y_links)):
+            for origin in range(2):
+                for k in range(4):
+                    value = y_first_recv[c, n, origin, pl.ds(k * local, local), :]
+                    y_recv[c, n, pl.ds(8 * k + origin * local, local), :] = value
 
     def carries(message, c):
         return [
@@ -261,16 +361,11 @@
 
     kept = jnp.where(chip == chips - 1, 0.0, 1.0)
 
-    def pack(message, load, pitch, base, first=None):
+    def pack(message, load, pitch, base, split=False):
         for n, (side, partner) in enumerate(x_links):
             for t in range(times):
                 value = load(pl.ds(t * pitch + base + side * (CELLS - 7), 4, stride=2))
                 x_send[message, n, pl.ds(4 * t, 4), :] = value
-            if first is not None:
-                value = value + kept * x_send[first, n, pl.ds(4 * (times - 1), 4), :]
-            x_send[message, n, pl.ds(4 * times, 4), :] = value
-            x_send[message, n, pl.ds(4 * times + 4, 4), :] = value
-            x_last[message, n] = value
         for n, (side, partner) in enumerate(y_links):
             for k in range(4):
                 total = None
@@ -279,13 +374,12 @@
                     value = load(pl.ds(row, times, stride=pitch))
                     value = pltpu.roll(value, lax.rem(BLOCK_EDGE * i + 128 - 112 * side, 128), 1)
                     total = value if total is None else jnp.where(flat_lane == i, value, total)
+                if split:
+                    for group in range(2):
+                        part = total[group * local : (group + 1) * local]
+                        y_first_send[message, n, group, pl.ds(k * local, local), :] = part
+                    continue
                 y_send[message, n, pl.ds(8 * k, times), :] = total
-                ending = total[times - 1 : times]
-                if first is not None:
-                    ending = ending + kept * y_send[first, n, pl.ds(8 * k + times - 1, 1), :]
-                y_send[message, n, pl.ds(32 + k, 1), :] = ending
-                y_send[message, n, pl.ds(36 + k, 1), :] = ending
-                y_last[message, n, pl.ds(k, 1), :] = ending
         for t in range(times):
             low = high = None
             for x in range(PLANES):
@@ -296,11 +390,30 @@
             pair = (pltpu.roll(low, 15, 1), high)
             for side in range(2):
                 z_send[message, side, pl.ds(8 * t, 8), :] = pair[side]
-                if t == times - 1:
-                    value = pair[side]
-                    if first is not None:
-                        value = value + kept * z_send[first, side, pl.ds(8 * t, 8), :]
-                    z_send[message, side, pl.ds(8 * times, 8), :] = value
+
+    def pack_last(message, load):
+        for n, (side, partner) in enumerate(x_links):
+            value = load(pl.ds(side * (CELLS - 7), 4, stride=2))
+            x_last[message, n] = value
+            x_send[message, n, pl.ds(4 * times, 4), :] = value
+            x_send[message, n, pl.ds(4 * times + 4, 4), :] = value
+        for n, (side, partner) in enumerate(y_links):
+            for k in range(4):
+                value = load(pl.ds(k % 2 * 64 + k // 2 + side * 6, 8, stride=8))
+                value = pltpu.roll(value, BLOCK_EDGE * side, 1)
+                value = pltpu.roll(value, 0, 1, stride=BLOCK_EDGE, stride_axis=0)
+                value = jnp.where(y_block == sub, value, 0.0)
+                value = jnp.sum(value, axis=0, keepdims=True)
+                y_last[message, n, pl.ds(k, 1), :] = value
+                y_send[message, n, pl.ds(32 + k, 1), :] = value
+                y_send[message, n, pl.ds(36 + k, 1), :] = value
+        low = high = None
+        for x in range(PLANES):
+            value = pltpu.roll(load(pl.ds(8 * x, 8)), (x - 15) % 128, 1)
+            high = value if high is None else jnp.where(z_index == x, value, high)
+            low = value if low is None else jnp.where(z_index == (x + 1) % 16, value, low)
+        z_send[message, 0, pl.ds(8 * times, 8), :] = pltpu.roll(low, 15, 1)
+        z_send[message, 1, pl.ds(8 * times, 8), :] = high
 
     wraps = [jnp.where(chip - j < 0, ALPHA_SCALE, 1.0) for j in range(1, chips + 1)]
     def gains_of(ratio):
@@ -489,6 +602,11 @@
 
         over_planes(plane)
 
+    def take(stage_ref, origin, store):
+        for j in range(local):
+            for q in range(half):
+                store(origin * local + j, q, stage_ref[q, pl.ds(j, ROWS, stride=local), :])
+
     def scatter(value, target, q):
         target[pl.ds(q, ROWS, stride=half), :] = value
 
@@ -542,34 +660,63 @@
     ghost_y[...] = jnp.zeros_like(ghost_y)
 
     pack(power_message, lambda at: power[at, :], WIDE, 0)
-    power_copies = copies(power_message, ends=False)
+    power_last = (times - 1) * WIDE
+    pack_last(power_message, lambda at: power[pl.ds(power_last + at.start, at.size, at.stride), :])
+
+    def offer(c):
+        owns[c].wait()
+        aways[c].wait()
+
+        def store_both(t, q, value):
+            field[c, pl.ds(t * TALL + 8 + q, ROWS, stride=half), :] = value
+            local_field[c, pl.ds(t * WIDE + q, ROWS, stride=half), :] = value
+
+        def store_away(t, q, value):
+            local_field[c, pl.ds(t * WIDE + q, ROWS, stride=half), :] = value
+
+        take(stage_iterate.at[core, :, c], core, store_both)
+        take(stage_away.at[:, c], 1 - core, store_away)
+        pack(c, lambda at: local_field[c, at, :], WIDE, 0, split=True)
+
+    offer(0)
+    pl.semaphore_wait(barrier, len(greet))
+    start_first(0)
+    for copy in swaps:
+        copy.start()
+    power_copies = halos(power_message)
     start_all(power_copies)
-
-    def take(stage_ref, store):
+    for c in range(1, COMPONENTS):
+        offer(c)
+        start_first(c)
+
+    def send_local(message, c):
+        pack_last(message, lambda at: end_send[c, at, :])
+        start_all(faces(message))
+        start_all(carries(message, c))
+        pack(message, lambda at: local_field[c, at, :], WIDE, 0)
+        start_all(halos(message))
+
+    def opening(c):
+        swaps[2 * c].wait()
+        swaps[2 * c + 1].wait()
+        owns[COMPONENTS + c].wait()
+
+        def store(t, q, value):
+            field[c, pl.ds(t * TALL + 8 + q, ROWS, stride=half), :] = value
+
+        def store_force(t, q, value):
+            force[c, pl.ds(t * CELLS + q, ROWS, stride=half), :] = value
+
+        take(stage_iterate.at[1 - core, :, c], 1 - core, store)
         for origin in range(2):
-            for j in range(local):
-                for q in range(half):
-                    store(origin * local + j, q, stage_ref[origin, q, pl.ds(j, ROWS, stride=local), :])
+            take(stage_forcing.at[origin, :, c], origin, store_force)
+        wait_first(c)
+        ghosts(c, c, "raw")
+        first_residual(c)
+        send_local(COMPONENTS + c, c)
 
     for c in range(COMPONENTS):
-        owns[c].wait()
-        swaps[c].wait()
-
-        def store(t, q, value, c=c):
-            field[c, pl.ds(t * TALL + 8 + q, ROWS, stride=half), :] = value
-
-        take(stage_iterate.at[:, :, c], store)
-        pack(c, lambda at, c=c: field[c, at, :], TALL, 8)
-        start_all(copies(c, ends=False))
-    for c in range(COMPONENTS):
-        owns[COMPONENTS + c].wait()
-        swaps[COMPONENTS + c].wait()
-
-        def store(t, q, value, c=c):
-            force[c, pl.ds(t * CELLS + q, ROWS, stride=half), :] = value
-
-        take(stage_forcing.at[:, :, c], store)
-
+        opening(c)
     wait_all(power_copies)
     for n in range(len(x_links)):
         for j, value in enumerate(gains_of(x_recv[power_message, n, pl.ds(4 * times, 4), :])):
@@ -582,24 +729,11 @@
         for j, value in enumerate(gains_of(ratio)):
             z_gain[side, j] = value
 
-    def send_local(message, c):
-        pack(message, lambda at: local_field[c, at, :], WIDE, 0, c)
-        start_all(copies(message))
-        start_all(carries(message, c))
-
-    def opening(c, carry):
-        wait_all(copies(c, ends=False))
-        ghosts(c, c, "raw")
-        first_residual(c)
-        send_local(COMPONENTS + c, c)
-        return carry
-
-    lax.fori_loop(0, COMPONENTS, opening, 0)
-
     def turn(step, carry):
         c = lax.rem(step, COMPONENTS)
         message = COMPONENTS + step
-        wait_all(copies(message))
+        wait_all(halos(message))
+        wait_all(faces(message))
         wait_all(carries(message, c))
         complete(message, c, False)
         ghosts(message, c, "next")
@@ -639,7 +773,8 @@
             return lambda held: held + local_field[c, at, :]
 
         give(c, stage_iterate, velocity, out_velocity, 2 * COMPONENTS + c)
-        wait_all(copies(message))
+        wait_all(halos(message))
+        wait_all(faces(message))
         ghosts(message, c, "last")
         last_residual(c)
 
@@ -713,6 +848,7 @@
         scratch_shapes=[
             stage,
             stage,
+            pltpu.VMEM((half, COMPONENTS, ROWS * local, LANES), f32),
             rows(COMPONENTS, times * TALL),
             rows(COMPONENTS, times * WIDE),
             rows(COMPONENTS, times * CELLS),
@@ -739,6 +875,8 @@
             rows(messages, 2, z_rows),
             rows(messages, nx, 4),
             rows(messages, ny, 4),
+            rows(COMPONENTS, ny, 2, 4 * local),
+            rows(COMPONENTS, ny, 2, 4 * local),
             rows(messages, nx, others, 4),
             rows(messages, ny, others, 4),
             rows(messages, 2, others, 8),
@@ -754,6 +892,7 @@
             pltpu.SemaphoreType.DMA((4 * COMPONENTS,)),
             pltpu.SemaphoreType.DMA((4 * COMPONENTS,)),
             pltpu.SemaphoreType.DMA((4 * COMPONENTS,)),
+            pltpu.SemaphoreType.DMA((COMPONENTS,)),
             pltpu.SemaphoreType.DMA((3,)),
         ],
         compiler_params=pltpu.CompilerParams(

time: 48.7 us -> 46.3 us (0.951)
  Pallas kernels: 47.9 us -> 45.5 us
    pallas_call x1, Pallas kernels: 46.2 us -> 43.8 us  [body(): pl.pallas_call(functools.partial(kernel, (chips, levels, slots, local)),...]
where the time goes in v4:
time: 46.3 us; the launch traced here: 46.1 us
  Pallas kernels  45.5 us (98%)
  between operations  0.64 us (1%)
    pallas_call x1, Pallas kernels, body(): pl.pallas_call(functools.partial(kernel, (chips, levels, slots, local)),...  43.8 us
    pallas_call x1, Pallas kernels, body(): pl.pallas_call(emit, out_shape=(shape, shape), in_specs=[pl.BlockSpec(mem...  1.68 us

profile of v4, /device:TPU:0, one launch (start us, length us, event | category | flops | bytes accessed | tf_op | source)
XLA Modules:
  0.0 46.1 jit_solution(922005759133026786)
XLA Ops:
  0.6 43.8 %shard_map.86 = (f32[8,3,128,128]{3,2,1,0:T(8,128)S(1)}, f32[8,3,128,128]{3,2,1,0:T(8,128)S(1)}) custom-call(s32[8,6]{1,0:T(8,128)} %holder.1, s32[8]{0:T(128)} %live.1, f32[8,3,128,128]{3,2,1,0:T(8,128)} %bitcast.29, f32[8,3,128,128]{3,2,1,0:T(8,128)} %bitcast.30, f32[3,32,8,128]{3,2,1,0:T(8,128)} %bitcast.31, f32[32,8,128]{2,1,0:T(8,128)} %bitcast.33, ...), custom_call_target="tpu_custom_call" | custom-call | tf_op jit(solution)/shard_map/pallas_call | solution.py:842
  44.4 1.7 %shard_map.87 = (f32[8,3,128,128]{3,2,1,0:T(8,128)}, f32[8,3,128,128]{3,2,1,0:T(8,128)}) custom-call(f32[8,3,128,128]{3,2,1,0:T(8,128)S(1)} %get-tuple-element.6.first, f32[8,3,128,128]{3,2,1,0:T(8,128)S(1)} %get-tuple-element.7.second), custom_call_target="tpu_custom_call" | custom-call | tf_op jit(solution)/shard_map/pallas_call | solution.py:913

commit v5 on v4

--- a/solution.py
+++ b/solution.py
@@ -19,6 +19,7 @@
 TALL = CELLS + 24
 WIDE = CELLS + 8
 UNROLL = 16
+ONCE = 16
 
 
 def kernel(
@@ -119,8 +120,10 @@
 
     x_links, y_links, z_links = links_of(0), links_of(1), links_of(2)
 
+    bases = [lax.rem(chip + jump, chips) * 2 for jump in range(chips)]
+
     def seat(jump, which):
-        return lax.rem(chip + jump, chips) * 2 + which
+        return bases[jump] + which
 
     greet = [{"tm": seat(j, core)} for j in range(1, chips)]
     for side, partner in x_links + y_links:
@@ -155,33 +158,31 @@
     mine = pl.ds(core * half, half)
     theirs = pl.ds((1 - core) * half, half)
     stage = (stage_send, stage_recv)
-    swaps, owns, aways = [], [], []
-    for c in range(COMPONENTS):
-        swaps.append(
-            remote(iterate.at[theirs, c], stage_iterate.at[core, :, c], stage, c, peer)
-        )
-        owns.append(
+
+    def swaps(c):
+        return [
+            remote(iterate.at[theirs, c], stage_iterate.at[core, :, c], stage, c, peer),
+            remote(forcing.at[theirs, c], stage_forcing.at[core, :, c], stage, COMPONENTS + c, peer),
+        ]
+
+    def owns(c):
+        return [
             pltpu.make_async_copy(
                 iterate.at[mine, c], stage_iterate.at[core, :, c], stage_local.at[c]
-            )
+            ),
+            pltpu.make_async_copy(iterate.at[theirs, c], stage_away.at[:, c], away_sem.at[c]),
+        ]
+
+    def own_forcing(c):
+        return pltpu.make_async_copy(
+            forcing.at[mine, c], stage_forcing.at[core, :, c], stage_local.at[COMPONENTS + c]
         )
-        aways.append(
-            pltpu.make_async_copy(iterate.at[theirs, c], stage_away.at[:, c], away_sem.at[c])
-        )
-        swaps.append(
-            remote(forcing.at[theirs, c], stage_forcing.at[core, :, c], stage, COMPONENTS + c, peer)
-        )
+
     for c in range(COMPONENTS):
-        owns.append(
-            pltpu.make_async_copy(
-                forcing.at[mine, c], stage_forcing.at[core, :, c], stage_local.at[COMPONENTS + c]
-            )
-        )
+        for copy in owns(c):
+            copy.start()
     for c in range(COMPONENTS):
-        owns[c].start()
-        aways[c].start()
-    for copy in owns[COMPONENTS:]:
-        copy.start()
+        own_forcing(c).start()
 
     per_message = (chips - 1) + chips * (len(x_links) + len(y_links) + 1 + len(z_links))
 
@@ -361,11 +362,13 @@
 
     kept = jnp.where(chip == chips - 1, 0.0, 1.0)
 
-    def pack(message, load, pitch, base, split=False):
+    def pack_x(message, load, pitch, base):
         for n, (side, partner) in enumerate(x_links):
             for t in range(times):
                 value = load(pl.ds(t * pitch + base + side * (CELLS - 7), 4, stride=2))
                 x_send[message, n, pl.ds(4 * t, 4), :] = value
+
+    def pack_y(message, load, pitch, base, split=False):
         for n, (side, partner) in enumerate(y_links):
             for k in range(4):
                 total = None
@@ -380,6 +383,8 @@
                         y_first_send[message, n, group, pl.ds(k * local, local), :] = part
                     continue
                 y_send[message, n, pl.ds(8 * k, times), :] = total
+
+    def pack_z(message, load, pitch, base):
         for t in range(times):
             low = high = None
             for x in range(PLANES):
@@ -390,6 +395,11 @@
             pair = (pltpu.roll(low, 15, 1), high)
             for side in range(2):
                 z_send[message, side, pl.ds(8 * t, 8), :] = pair[side]
+
+    def pack(message, load, pitch, base, split=False):
+        pack_z(message, load, pitch, base)
+        pack_y(message, load, pitch, base, split)
+        pack_x(message, load, pitch, base)
 
     def pack_last(message, load):
         for n, (side, partner) in enumerate(x_links):
@@ -518,14 +528,14 @@
         high = jnp.where(z_last, edge, pltpu.roll(value, 127, 1))
         return value, total + factors[4] * low + factors[5] * high
 
-    def over_planes(body):
+    def over_planes(body, unroll=ONCE):
         def one(group, carry):
-            for i in range(UNROLL):
-                x = group * UNROLL + i
+            for i in range(unroll):
+                x = group * unroll + i
                 body(x, pl.multiple_of(x * 8, 8), i % 2)
             return carry
 
-        lax.fori_loop(0, PLANES // UNROLL, one, 0)
+        lax.fori_loop(0, PLANES // unroll, one, 0)
 
     def factors_at(row):
         return [coefficient[f, pl.ds(row, 8), :] for f in range(6)]
@@ -544,7 +554,7 @@
                 before = total
             end_send[c, pl.ds(row, 8), :] = before + carry[c, pl.ds(row, 8), :]
 
-        over_planes(plane)
+        over_planes(plane, UNROLL)
 
     def first_residual(c):
         def plane(x, row, parity):
@@ -664,8 +674,8 @@
     pack_last(power_message, lambda at: power[pl.ds(power_last + at.start, at.size, at.stride), :])
 
     def offer(c):
-        owns[c].wait()
-        aways[c].wait()
+        for copy in owns(c):
+            copy.wait()
 
         def store_both(t, q, value):
             field[c, pl.ds(t * TALL + 8 + q, ROWS, stride=half), :] = value
@@ -681,25 +691,40 @@
     offer(0)
     pl.semaphore_wait(barrier, len(greet))
     start_first(0)
-    for copy in swaps:
-        copy.start()
+    for c in range(COMPONENTS):
+        for copy in swaps(c):
+            copy.start()
     power_copies = halos(power_message)
     start_all(power_copies)
-    for c in range(1, COMPONENTS):
+
+    def offering(c, carry):
         offer(c)
         start_first(c)
+        return carry
+
+    lax.fori_loop(1, COMPONENTS, offering, 0)
 
     def send_local(message, c):
         pack_last(message, lambda at: end_send[c, at, :])
         start_all(faces(message))
         start_all(carries(message, c))
-        pack(message, lambda at: local_field[c, at, :], WIDE, 0)
-        start_all(halos(message))
-
-    def opening(c):
-        swaps[2 * c].wait()
-        swaps[2 * c + 1].wait()
-        owns[COMPONENTS + c].wait()
+        found = halos(message)
+        first, second = len(x_links), len(x_links) + len(y_links)
+
+        def load(at):
+            return local_field[c, at, :]
+
+        pack_z(message, load, WIDE, 0)
+        start_all(found[second:])
+        pack_y(message, load, WIDE, 0)
+        start_all(found[first:second])
+        pack_x(message, load, WIDE, 0)
+        start_all(found[:first])
+
+    def opening(c, carry):
+        for copy in swaps(c):
+            copy.wait()
+        own_forcing(c).wait()
 
         def store(t, q, value):
             field[c, pl.ds(t * TALL + 8 + q, ROWS, stride=half), :] = value
@@ -714,9 +739,9 @@
         ghosts(c, c, "raw")
         first_residual(c)
         send_local(COMPONENTS + c, c)
-
-    for c in range(COMPONENTS):
-        opening(c)
+        return carry
+
+    lax.fori_loop(0, COMPONENTS, opening, 0)
     wait_all(power_copies)
     for n in range(len(x_links)):
         for j, value in enumerate(gains_of(x_recv[power_message, n, pl.ds(4 * times, 4), :])):
@@ -743,48 +768,58 @@
 
     lax.fori_loop(0, COMPONENTS * (SWEEPS - 1), turn, 0)
 
-    finals = []
-
-    def give(c, stage_ref, load, out, number):
+    def giving(c, stage_ref, out, number):
+        away = remote(
+            stage_ref.at[1 - core, :, c], out.at[mine, c], stage, number + c, peer
+        )
+        here = pltpu.make_async_copy(
+            stage_ref.at[core, :, c], out.at[mine, c], stage_local.at[number + c]
+        )
+        return [away, here]
+
+    def fill(c, stage_ref, load, added):
         for origin in range(2):
             for j in range(local):
                 for q in range(half):
                     value = load(origin * local + j, q)
                     at = pl.ds(j, ROWS, stride=local)
-                    value = value(stage_ref[origin, q, c, at, :])
+                    if added:
+                        value = value + stage_ref[origin, q, c, at, :]
                     stage_ref[origin, q, c, at, :] = value
-        away = remote(
-            stage_ref.at[1 - core, :, c], out.at[mine, c], stage, number, peer
-        )
-        here = pltpu.make_async_copy(
-            stage_ref.at[core, :, c], out.at[mine, c], stage_local.at[number]
-        )
-        away.start()
-        here.start()
-        finals.extend([away, here])
-
-    for c in range(COMPONENTS):
+
+    gives = ((stage_iterate, out_velocity, 2 * COMPONENTS), (stage_forcing, out_residual, 3 * COMPONENTS))
+
+    def closing(c, carry):
         message = COMPONENTS * SWEEPS + c
         wait_all(carries(message, c))
         complete(message, c, True)
-
-        def velocity(t, q, c=c):
-            at = pl.ds(t * WIDE + q, ROWS, stride=half)
-            return lambda held: held + local_field[c, at, :]
-
-        give(c, stage_iterate, velocity, out_velocity, 2 * COMPONENTS + c)
+        fill(
+            c,
+            stage_iterate,
+            lambda t, q: local_field[c, pl.ds(t * WIDE + q, ROWS, stride=half), :],
+            True,
+        )
+        for copy in giving(c, *gives[0]):
+            copy.start()
         wait_all(halos(message))
         wait_all(faces(message))
         ghosts(message, c, "last")
         last_residual(c)
-
-        def remainder(t, q, c=c):
-            at = pl.ds(t * CELLS + q, ROWS, stride=half)
-            return lambda held: source[c, at, :]
-
-        give(c, stage_forcing, remainder, out_residual, 3 * COMPONENTS + c)
-    for copy in finals:
-        copy.wait()
+        fill(
+            c,
+            stage_forcing,
+            lambda t, q: source[c, pl.ds(t * CELLS + q, ROWS, stride=half), :],
+            False,
+        )
+        for copy in giving(c, *gives[1]):
+            copy.start()
+        return carry
+
+    lax.fori_loop(0, COMPONENTS, closing, 0)
+    for c in range(COMPONENTS):
+        for give in gives:
+            for copy in giving(c, *give):
+                copy.wait()
 
 
 def emit(first, second, first_out, second_out, sem):

time: 46.3 us -> 46.1 us (level)
  no operation moved by 1% of the time
where the time goes in v5:
time: 46.1 us; the launch traced here: 45.9 us
  Pallas kernels  45.3 us (98%)
  between operations  0.64 us (1%)
    pallas_call x1, Pallas kernels, body(): pl.pallas_call(functools.partial(kernel, (chips, levels, slots, local)),...  43.6 us
    pallas_call x1, Pallas kernels, body(): pl.pallas_call(emit, out_shape=(shape, shape), in_specs=[pl.BlockSpec(mem...  1.68 us

profile of v5, /device:TPU:0, one launch (start us, length us, event | category | flops | bytes accessed | tf_op | source)
XLA Modules:
  0.0 45.9 jit_solution(7299479399600775522)
XLA Ops:
  0.6 43.6 %shard_map.86 = (f32[8,3,128,128]{3,2,1,0:T(8,128)S(1)}, f32[8,3,128,128]{3,2,1,0:T(8,128)S(1)}) custom-call(s32[8,6]{1,0:T(8,128)} %holder.1, s32[8]{0:T(128)} %live.1, f32[8,3,128,128]{3,2,1,0:T(8,128)} %bitcast.29, f32[8,3,128,128]{3,2,1,0:T(8,128)} %bitcast.30, f32[3,32,8,128]{3,2,1,0:T(8,128)} %bitcast.31, f32[32,8,128]{2,1,0:T(8,128)} %bitcast.33, ...), custom_call_target="tpu_custom_call" | custom-call | tf_op jit(solution)/shard_map/pallas_call | solution.py:877
  44.3 1.7 %shard_map.87 = (f32[8,3,128,128]{3,2,1,0:T(8,128)}, f32[8,3,128,128]{3,2,1,0:T(8,128)}) custom-call(f32[8,3,128,128]{3,2,1,0:T(8,128)S(1)} %get-tuple-element.6.first, f32[8,3,128,128]{3,2,1,0:T(8,128)S(1)} %get-tuple-element.7.second), custom_call_target="tpu_custom_call" | custom-call | tf_op jit(solution)/shard_map/pallas_call | solution.py:948
